TPU v7x, 32 devices: a whole 2x2x4 slice. The times are simulated.
32 devices in a mesh: group: 8 (over y, x, core), section: 4 (over z).
Axes of the slice: x: 2, y: 2, z: 4, core: 2. Of those that a mesh axis runs over, the one named last changes fastest.
Arguments:
- columns: float32 [8, 8, 16, 8192], P('group', None, None, 'section'), may hold values from -6 to 6
- vectors: bfloat16 [8, 8, 128, 8192], P('group', None, None, 'section'), may hold values from -0.0625 to 0.0625
- factors: float32 [8, 8, 128, 128], P('group'), as said below
- order: int32 [8], P('group'), may hold values from 4096 to 8192
- blocks: int32 [8], P('group'), may hold values from 1 to 8
- live: int32 [8, 8], P('group'), may hold values from 0 to 16
Outputs:
- result: float32 [8, 8, 16, 8192], P('group', None, None, 'section')
Inputs may be any that keep to these rules, and one draw needn't show every extreme that they name: `factors`: upper triangular, diagonal entries between one half and two, off-diagonal entries small.
All inputs are finite; a program needn't handle non-finite values.
Results may differ from a plain program's by a relative error of at most 0.0003.
Values sent between devices are 32-bit elements; how exact they have to be, the bound alone decides.
No kernel may reach another device: no remote copies, remote signals or barrier semaphores. Data moves between devices by JAX's collectives and lax.ppermute only.
A program may use at most 64 MiB of HBM per device.

v0:
```python
import jax
import jax.numpy as jnp
from jax import lax
from jax.sharding import PartitionSpec as P


def shards(columns, vectors, factors, order, blocks, live):
    count = vectors.shape[1]
    width = vectors.shape[2]
    rows = vectors.shape[3]
    slots = columns.shape[2]
    first_row = lax.axis_index("section") * rows
    inside = (first_row + jnp.arange(rows) < order[0]).astype(jnp.float32)
    basis_all = vectors[0].astype(jnp.float32) * inside[None, None, :]
    active = (jnp.arange(count) < blocks[0]).astype(jnp.float32)
    factor_all = factors[0] * active[:, None, None]
    high = lax.Precision.HIGHEST
    local_correlation = jnp.einsum("jar,jbr->jab", basis_all[0::2], basis_all[1::2], precision=high)
    correlation_all = lax.psum(local_correlation, "section")
    merged = []
    zeros = jnp.zeros((width, width), jnp.float32)
    for pair in range(count // 2):
        upper_t = factor_all[2 * pair]
        lower_t = factor_all[2 * pair + 1]
        corner = -jnp.dot(
            jnp.dot(upper_t, correlation_all[pair], precision=high), lower_t, precision=high
        )
        top = jnp.concatenate([upper_t, corner], axis=1)
        bottom = jnp.concatenate([zeros, lower_t], axis=1)
        joined = jnp.concatenate([basis_all[2 * pair], basis_all[2 * pair + 1]], axis=0)
        merged.append((joined, jnp.concatenate([top, bottom], axis=0)))
    held = lax.all_to_all(columns[0], "group", split_axis=0, concat_axis=0, tiled=True)
    shape = held.shape
    panel = held.reshape(shape[0] * shape[1], shape[2])
    transform_panel = panel
    for pair in reversed(range(count // 2)):
        joined, factor = merged[pair]
        inner = lax.psum(jnp.dot(transform_panel, joined.T, precision=high), "section")
        scaled = jnp.dot(inner, factor.T, precision=high)
        transform_panel = transform_panel - jnp.dot(scaled, joined, precision=high)
    moved = transform_panel.reshape(shape)
    returned = lax.all_to_all(moved, "group", split_axis=0, concat_axis=0, tiled=True)
    keep = jnp.arange(slots)[None, :] < live[0][:, None]
    return jnp.where(keep[:, :, None], returned, jnp.float32(0.0))[None]


def solution(mesh):
    return jax.shard_map(
        shards,
        mesh=mesh,
        in_specs=(
            P("group", None, None, "section"),
            P("group", None, None, "section"),
            P("group", None, None, None),
            P("group"),
            P("group"),
            P("group", None),
        ),
        out_specs=P("group", None, None, "section"),
        check_vma=False,
    )
```

profile of v0, /device:TPU:0, one launch (start us, length us, event | category | flops | bytes accessed | tf_op | source)
XLA Modules:
  0.0 233.6 jit_solution(4334425276789696389)
XLA Ops:
  6.5 5.2 %all-to-all-start = ((f32[8,16,2048]{2,1,0:T(8,128)}), f32[8,16,2048]{2,1,0:T(8,128)}, u32[]{:S(2)}, u32[]{:S(2)}) async-start(f32[8,16,2048]{2,1,0:T(8,128)} %bitcast.85), calls=%async_computation | async-start | bytes 2097152 | tf_op jit(solution)/shard_map/all_to_all | solution.py:32
  12.4 3.4 %convert_multiply_fusion = f32[8,128,2048]{2,1,0:T(8,128)S(1)} fusion(bf16[1,8,128,2048]{3,2,1,0:T(8,128)(2,1)} %param.7, f32[2048]{0:T(1024)S(1)} %fusion.40), kind=kLoop, calls=%fused_computation | loop fusion | flops 4194304 | bytes 12591104 | tf_op jit(solution)/shard_map/mul | solution.py:14
  15.8 4.7 %fusion = f32[4,128,128]{2,1,0:T(8,128)} fusion(f32[8,128,2048]{2,1,0:T(8,128)S(1)} %convert_multiply_fusion), kind=kOutput, calls=%fused_computation.1 | convolution fusion | flops 1610612736 | bytes 8650752 | tf_op jit(solution)/shard_map/jar,jbr->jab/dot_general | solution.py:18
  21.1 2.5 %slice_bitcast_fusion.1 = (f32[128,2048]{1,0:T(8,128)S(1)}, f32[128,2048]{1,0:T(8,128)S(1)}, f32[128,2048]{1,0:T(8,128)}, f32[128,2048]{1,0:T(8,128)}, f32[128,2...) fusion(f32[8,128,2048]{2,1,0:T(8,128)S(1)} %convert_multiply_fusion), kind=kLoop, calls=%fused_computation.22 | loop fusion | bytes 16777216 | tf_op jit(solution)/shard_map/squeeze | solution.py:30
  23.6 3.6 %all-to-all-done = f32[8,16,2048]{2,1,0:T(8,128)} async-done(((f32[8,16,2048]{2,1,0:T(8,128)}), f32[8,16,2048]{2,1,0:T(8,128)}, u32[]{:S(2)}, u32[]{:S(2)}) %all-to-all-start) | async-done | bytes 1048608 | tf_op jit(solution)/shard_map/all_to_all | solution.py:32
  27.2 4.3 %fusion.7 = f32[128,256]{0,1:T(8,128)} fusion(f32[128,2048]{1,0:T(8,128)} %bitcast.2, f32[128,2048]{1,0:T(8,128)} %get-tuple-element.13, f32[128,2048]{1,0:T(8,128)} %get-tuple-element.14), kind=kOutput, calls=%fused_computation.16 | convolution fusion | flops 805830656 | bytes 3276800 | tf_op jit(solution)/shard_map/dot_general | solution.py:38
  31.6 1.1 bitcast_multiply_fusion
  34.3 34.2 %all-reduce.16.cloned.1.call-done = (f32[128,256]{0,1:T(8,128)}, f32[4,128,128]{2,1,0:T(8,128)}) async-done(((f32[128,256]{0,1:T(8,128)}, f32[4,128,128]{2,1,0:T(8,128)}), (f32[128,256]{0,1:T(8,128)}, f32[4,128,128]{2,1,0:T(8,128)})) %all-reduce.16.cloned.1.call-update) | async-done | bytes 393232 | tf_op jit(solution)/shard_map/psum | solution.py:38
  68.5 1.2 fusion.39
  69.7 1.1 fusion.38
  70.8 1.1 fusion.37
  71.9 1.1 fusion.36
  74.0 1.3 fusion.14
  75.4 2.9 %convolution_subtract_fusion.3 = f32[128,2048]{1,0:T(8,128)S(1)} fusion(f32[128,2048]{1,0:T(8,128)} %bitcast.2, f32[128,256]{1,0:T(8,128)S(1)} %fusion.14, f32[128,2048]{1,0:T(8,128)S(1)} %copy-done.3, f32[128,2048]{1,0:T(8,128)} %get-tuple-element.14), kind=kOutput, calls=%fused_computation.7 | convolution fusion | flops 806092800 | bytes 4325376 | tf_op jit(solution)/shard_map/dot_general | solution.py:40
  79.3 2.9 %fusion.5 = f32[128,256]{1,0:T(8,128)} fusion(f32[128,2048]{1,0:T(8,128)S(1)} %convolution_subtract_fusion.3, f32[128,2048]{1,0:T(8,128)S(1)} %copy-done.1, f32[128,2048]{1,0:T(8,128)S(1)} %copy-done.2), kind=kOutput, calls=%fused_computation.14 | convolution fusion | flops 805830656 | bytes 3276800 | tf_op jit(solution)/shard_map/dot_general | solution.py:38
  82.4 1.7 convolution_negate_fusion.2
  84.1 32.7 %all-reduce.10.cloned.1.call-done = f32[128,256]{1,0:T(8,128)} async-done(((f32[128,256]{1,0:T(8,128)}), f32[128,256]{1,0:T(8,128)}) %all-reduce.10.cloned.1.call-update) | async-done | bytes 131088 | tf_op jit(solution)/shard_map/psum | solution.py:38
  116.7 1.4 fusion.12
  118.1 3.2 %convolution_subtract_fusion.2 = f32[128,2048]{1,0:T(8,128)S(1)} fusion(f32[128,2048]{1,0:T(8,128)} %copy-done.5, f32[128,256]{1,0:T(8,128)S(1)} %fusion.12, f32[128,2048]{1,0:T(8,128)} %get-tuple-element.10, f32[128,2048]{1,0:T(8,128)} %get-tuple-element.11), kind=kOutput, calls=%fused_computation.6 | convolution fusion | flops 806092800 | bytes 4325376 | tf_op jit(solution)/shard_map/dot_general | solution.py:40
  122.3 2.9 %fusion.4 = f32[128,256]{1,0:T(8,128)} fusion(f32[128,2048]{1,0:T(8,128)S(1)} %convolution_subtract_fusion.2, f32[128,2048]{1,0:T(8,128)S(1)} %get-tuple-element.8, f32[128,2048]{1,0:T(8,128)S(1)} %copy-done), kind=kOutput, calls=%fused_computation.13 | convolution fusion | flops 805830656 | bytes 3276800 | tf_op jit(solution)/shard_map/dot_general | solution.py:38
  125.2 1.7 convolution_negate_fusion.1
  126.9 32.7 %all-reduce.12.cloned.1.call-done = f32[128,256]{1,0:T(8,128)} async-done(((f32[128,256]{1,0:T(8,128)}), f32[128,256]{1,0:T(8,128)}) %all-reduce.12.cloned.1.call-update) | async-done | bytes 131088 | tf_op jit(solution)/shard_map/psum | solution.py:38
  159.7 1.3 fusion.10
  161.0 2.8 %convolution_subtract_fusion.1 = f32[128,2048]{1,0:T(8,128)S(1)} fusion(f32[128,2048]{1,0:T(8,128)} %copy-done.6, f32[128,256]{1,0:T(8,128)S(1)} %fusion.10, f32[128,2048]{1,0:T(8,128)S(1)} %get-tuple-element.8, f32[128,2048]{1,0:T(8,128)} %get-tuple-element.9), kind=kOutput, calls=%fused_computation.5 | convolution fusion | flops 806092800 | bytes 4325376 | tf_op jit(solution)/shard_map/dot_general | solution.py:40
  164.7 2.9 %fusion.3 = f32[128,256]{1,0:T(8,128)} fusion(f32[128,2048]{1,0:T(8,128)S(1)} %convolution_subtract_fusion.1, f32[128,2048]{1,0:T(8,128)S(1)} %get-tuple-element.12, f32[128,2048]{1,0:T(8,128)S(1)} %get-tuple-element.7), kind=kOutput, calls=%fused_computation.12 | convolution fusion | flops 805830656 | bytes 3276800 | tf_op jit(solution)/shard_map/dot_general | solution.py:38
  167.6 1.0 convolution_negate_fusion
  168.7 33.4 %all-reduce.14.cloned.1.call-done = f32[128,256]{1,0:T(8,128)} async-done(((f32[128,256]{1,0:T(8,128)}), f32[128,256]{1,0:T(8,128)}) %all-reduce.14.cloned.1.call-update) | async-done | bytes 131088 | tf_op jit(solution)/shard_map/psum | solution.py:38
  202.1 1.3 fusion.8
  203.4 3.4 %convolution_subtract_fusion = f32[128,2048]{1,0:T(8,128)} fusion(f32[128,2048]{1,0:T(8,128)} %copy-done.4, f32[128,256]{1,0:T(8,128)S(1)} %fusion.8, f32[128,2048]{1,0:T(8,128)S(1)} %get-tuple-element.12, f32[128,2048]{1,0:T(8,128)S(1)} %get-tuple-element.7), kind=kOutput, calls=%fused_computation.4 | convolution fusion | flops 806092800 | bytes 4325376 | tf_op jit(solution)/shard_map/dot_general | solution.py:40
  206.9 3.8 %all-to-all-start.1 = ((f32[8,16,2048]{2,1,0:T(8,128)}), f32[8,16,2048]{2,1,0:T(8,128)S(1)}, u32[]{:S(2)}, u32[]{:S(2)}) async-start(f32[8,16,2048]{2,1,0:T(8,128)} %bitcast.28), calls=%async_computation.1 | async-start | bytes 2097152 | tf_op jit(solution)/shard_map/all_to_all | solution.py:42
  210.7 15.3 %all-to-all-done.1 = f32[8,16,2048]{2,1,0:T(8,128)S(1)} async-done(((f32[8,16,2048]{2,1,0:T(8,128)}), f32[8,16,2048]{2,1,0:T(8,128)S(1)}, u32[]{:S(2)}, u32[]{:S(2)}) %all-to-all-start.1) | async-done | bytes 1048608 | tf_op jit(solution)/shard_map/all_to_all | solution.py:42
  226.0 1.1 select_bitcast_fusion
  (33 shorter events, 6.0 us)
Async XLA Ops:
  6.5 20.7 %all-to-all-start = ((f32[8,16,2048]{2,1,0:T(8,128)}), f32[8,16,2048]{2,1,0:T(8,128)}, u32[]{:S(2)}, u32[]{:S(2)}) async-start(f32[8,16,2048]{2,1,0:T(8,128)} %bitcast.85), calls=%async_computation | async-start | bytes 2097152 | tf_op jit(solution)/shard_map/all_to_all | solution.py:32
  11.7 56.8 %all-reduce.16.cloned.1.call-start = ((), (), s32[]{:S(2)}) async-start(), calls=%async_computation.5 | async-start | bytes 786432 | tf_op jit(solution)/shard_map/psum | solution.py:38
  31.5 85.2 %all-reduce.10.cloned.1.call-start = ((), (), s32[]{:S(2)}) async-start(), calls=%async_computation.2 | async-start | bytes 262144 | tf_op jit(solution)/shard_map/psum | solution.py:38
  32.7 0.8 copy-start.7
  68.5 6.8 %copy-start.3 = (f32[128,2048]{1,0:T(8,128)S(1)}, f32[128,2048]{1,0:T(8,128)}, u32[]{:S(2)}) copy-start(f32[128,2048]{1,0:T(8,128)} %get-tuple-element.13) | copy-start | bytes 3145732
  75.3 3.9 %copy-start.1 = (f32[128,2048]{1,0:T(8,128)S(1)}, f32[128,2048]{1,0:T(8,128)}, u32[]{:S(2)}) copy-start(f32[128,2048]{1,0:T(8,128)} %get-tuple-element.10) | copy-start | bytes 3145732
  75.3 3.9 %copy-start.2 = (f32[128,2048]{1,0:T(8,128)S(1)}, f32[128,2048]{1,0:T(8,128)}, u32[]{:S(2)}) copy-start(f32[128,2048]{1,0:T(8,128)} %get-tuple-element.11) | copy-start | bytes 3145732
  78.3 1.0 copy-start.5
  82.2 77.5 %all-reduce.12.cloned.1.call-start = ((), (), s32[]{:S(2)}) async-start(), calls=%async_computation.3 | async-start | bytes 262144 | tf_op jit(solution)/shard_map/psum | solution.py:38
  118.1 4.2 %copy-start = (f32[128,2048]{1,0:T(8,128)S(1)}, f32[128,2048]{1,0:T(8,128)}, u32[]{:S(2)}) copy-start(f32[128,2048]{1,0:T(8,128)} %get-tuple-element.9) | copy-start | bytes 3145732
  121.3 1.0 copy-start.6
  121.3 38.3 %copy-start.8 = (f32[128,128]{1,0:T(8,128)S(1)}, f32[128,128]{1,0:T(8,128)}, u32[]{:S(2)}) copy-start(f32[128,128]{1,0:T(8,128)} %get-tuple-element.18) | copy-start | bytes 196612
  125.2 76.9 %all-reduce.14.cloned.1.call-start = ((), (), s32[]{:S(2)}) async-start(), calls=%async_computation.4 | async-start | bytes 262144 | tf_op jit(solution)/shard_map/psum | solution.py:38
  163.8 1.0 copy-start.4
  206.9 3.8 %copy-start.9 = (s32[1,8]{1,0:T(1,128)S(1)}, s32[1,8]{1,0:T(1,128)}, u32[]{:S(2)}) copy-start(s32[1,8]{1,0:T(1,128)} %param.11) | copy-start | bytes 100
  206.9 19.1 %all-to-all-start.1 = ((f32[8,16,2048]{2,1,0:T(8,128)}), f32[8,16,2048]{2,1,0:T(8,128)S(1)}, u32[]{:S(2)}, u32[]{:S(2)}) async-start(f32[8,16,2048]{2,1,0:T(8,128)} %bitcast.28), calls=%async_computation.1 | async-start | bytes 2097152 | tf_op jit(solution)/shard_map/all_to_all | solution.py:42
Sparse Core Ops, SparseCore 0:
  31.7 36.8 all-reduce.15
  82.3 34.4 all-reduce.9
  125.3 34.2 all-reduce.11
  167.8 34.2 all-reduce.13
where the time goes:
time: 234 us
  waiting for transfers between devices  152 us (65%)
  matrix products  45.1 us (19%)
  between operations  14.7 us (6%)
  starting transfers between devices  9.31 us (4%)
  local copies, waits for them, and re-layouts  6.94 us (3%)
  other arithmetic  5.71 us (2%)
    psum x4, waiting for transfers between devices, shards(): lax.psum(jnp.dot(transform_panel, joined.T, precision=high), 'section')  133 us
    all_to_all x1, waiting for transfers between devices, shards(): lax.all_to_all(moved, 'group', split_axis=0, concat_axis=0, tiled=True)  15.3 us
    dot_general x4, matrix products, shards(): jnp.dot(transform_panel, joined.T, precision=high)  12.9 us
    dot_general x4, matrix products, shards(): transform_panel = transform_panel - jnp.dot(scaled, joined, precision=high)  12.3 us
    dot_general x4, matrix products, shards(): jnp.dot(jnp.dot(upper_t, correlation_all[pair], precision=high), lower_t,...  5.47 us
    dot_general x4, matrix products, shards(): scaled = jnp.dot(inner, factor.T, precision=high)  5.29 us
    all_to_all x1, starting transfers between devices, shards(): lax.all_to_all(columns[0], 'group', split_axis=0, concat_axis=0, tiled=True)  5.2 us
  transfers between devices with their start and end apart: 6, of which 6 were waited for; matrix products, arithmetic and copies ran while one was open for 7% of the time, Pallas kernels for 0%

commit v1 on v0

v1 whole, which is shorter than its diff:
```python
import jax
import jax.numpy as jnp
from jax import lax
from jax.sharding import PartitionSpec as P

HIGH = lax.Precision.HIGHEST
PER_ROUND = 2


def total(value, axis):
    count = lax.axis_size(axis)
    if count & (count - 1):
        return lax.psum(value, axis)
    step = 1
    while step < count:
        value = value + lax.ppermute(value, axis, [(i, i ^ step) for i in range(count)])
        step *= 2
    return value


def split(value):
    upper = lax.reduce_precision(value, 8, 7)
    return upper.astype(jnp.bfloat16), (value - upper).astype(jnp.bfloat16)


def contract(left, right, dims):
    return lax.dot_general(left, right, (dims, ((), ())), preferred_element_type=jnp.float32)


def shards(columns, vectors, factors, order, blocks, live):
    count, width, rows = vectors.shape[1:]
    slots = columns.shape[2]
    held = lax.all_to_all(columns[0], "group", split_axis=0, concat_axis=0, tiled=True)
    shape = held.shape
    panel = held.reshape(shape[0] * shape[1], rows)

    first_row = lax.axis_index("section") * rows
    inside = first_row + jnp.arange(rows) < order[0]
    basis = jnp.where(inside[None, None, :], vectors[0], jnp.bfloat16(0)).reshape(count * width, rows)
    active = (jnp.arange(count) < blocks[0]).astype(jnp.float32)
    factor = factors[0] * active[:, None, None]

    groups = [range(max(top - PER_ROUND, 0), top) for top in range(count, 0, -PER_ROUND)]
    spans = [slice(g.start * width, g.stop * width) for g in groups]

    pieces, where = [], []
    for g in groups:
        for low in g:
            for high in range(low + 1, g.stop):
                where.append((low, high))
                pieces.append(contract(
                    basis[low * width:(low + 1) * width], basis[high * width:(high + 1) * width], ((1,), (1,))))
    inner_gram = dict(zip(where, total(jnp.stack(pieces), "section")))

    merged = []
    for g in groups:
        table = {}
        for low in reversed(g):
            table[low, low] = factor[low]
            for high in range(low + 1, g.stop):
                acc = sum(
                    jnp.dot(inner_gram[low, mid], table[mid, high], precision=HIGH)
                    for mid in range(low + 1, high + 1))
                table[low, high] = -jnp.dot(factor[low], acc, precision=HIGH)
        zero = jnp.zeros((width, width), jnp.float32)
        merged.append(jnp.concatenate(
            [jnp.concatenate([table.get((a, b), zero) for b in g], axis=1) for a in g], axis=0))

    upper, lower = split(panel)
    both = jnp.concatenate([upper, lower], axis=0)
    twice = contract(both, basis, ((1,), (1,)))
    first = twice[:panel.shape[0]] + twice[panel.shape[0]:]

    done = []
    for index, span in enumerate(spans):
        partial = first[:, span]
        if index:
            cross = contract(basis[span], basis[span.stop:], ((1,), (1,)))
            known = jnp.concatenate(done[::-1], axis=1)
            partial = partial - lax.dot_general(known, cross, (((1,), (1,)), ((), ())), precision=HIGH)
        inner = total(partial, "section")
        done.append(lax.dot_general(inner, merged[index], (((1,), (1,)), ((), ())), precision=HIGH))
    weights = jnp.concatenate(done[::-1], axis=1)
    upper, lower = split(weights)
    update = contract(jnp.concatenate([upper, lower], axis=0), basis, ((1,), (0,)))
    moved = (panel - update[:panel.shape[0]] - update[panel.shape[0]:]).reshape(shape)
    returned = lax.all_to_all(moved, "group", split_axis=0, concat_axis=0, tiled=True)
    keep = jnp.arange(slots)[None, :] < live[0][:, None]
    return jnp.where(keep[:, :, None], returned, jnp.float32(0.0))[None]


def solution(mesh):
    return jax.shard_map(
        shards,
        mesh=mesh,
        in_specs=(
            P("group", None, None, "section"),
            P("group", None, None, "section"),
            P("group", None, None, None),
            P("group"),
            P("group"),
            P("group", None),
        ),
        out_specs=P("group", None, None, "section"),
        check_vma=False,
    )
```

time: 234 us -> 124 us (0.53)
  waiting for transfers between devices: 152 us -> 79.1 us
  matrix products: 45.1 us -> 14.2 us
  between operations: 14.7 us -> 1.91 us
  starting transfers between devices: 9.31 us -> 14.7 us
  other arithmetic: 5.71 us -> 10.7 us
  local copies, waits for them, and re-layouts: 6.94 us -> 3.15 us
    psum x4 -> x0, waiting for transfers between devices: 133 us -> none  [shards(): lax.psum(jnp.dot(transform_panel, joined.T, precision=high), 'section')]
    ppermute x0 -> x10, waiting for transfers between devices: none -> 63.8 us  [total(): lax.ppermute(value, axis, [(i, i ^ step) for i in range(count)])]
    dot_general x21 -> x24, matrix products: 45.1 us -> 14.2 us  [the longest x9 9.03 us: contract(): lax.dot_general(left, right, (dims, ((), ())), preferred_element_type=jnp...]
    ppermute x0 -> x10, starting transfers between devices: none -> 7.4 us  [total(): lax.ppermute(value, axis, [(i, i ^ step) for i in range(count)])]
    select_n x0 -> x2, other arithmetic: none -> 7.04 us  [shards(): jnp.where(inside[None, None, :], vectors[0], jnp.bfloat16(0))]
    mul x2 -> x1, other arithmetic: 4.52 us -> 0.1 us  [shards(): factor = factors[0] * active[:, None, None]]
    all_to_all x1, waiting for transfers between devices: 3.61 us -> 0.01 us  [shards(): lax.all_to_all(columns[0], 'group', split_axis=0, concat_axis=0, tiled=True)]
    unnamed x20 -> x24, local copies, waits for them, and re-layouts: 3.74 us -> 1.15 us
  transfers between devices with their start and end apart: 6 -> 12, of which waited for: 6 -> 10; matrix products, arithmetic and copies ran while one was open for 7% -> 9% of each run, Pallas kernels for 0% -> 0%
where the time goes in v1:
time: 124 us
  waiting for transfers between devices  79.1 us (64%)
  starting transfers between devices  14.7 us (12%)
  matrix products  14.2 us (11%)
  other arithmetic  10.7 us (9%)
  local copies, waits for them, and re-layouts  3.15 us (3%)
  between operations  1.91 us (2%)
    ppermute x10, waiting for transfers between devices, total(): lax.ppermute(value, axis, [(i, i ^ step) for i in range(count)])  63.8 us
    all_to_all x1, waiting for transfers between devices, shards(): lax.all_to_all(moved, 'group', split_axis=0, concat_axis=0, tiled=True)  15.3 us
    dot_general x9, matrix products, contract(): lax.dot_general(left, right, (dims, ((), ())), preferred_element_type=jnp...  9.03 us
    ppermute x10, starting transfers between devices, total(): lax.ppermute(value, axis, [(i, i ^ step) for i in range(count)])  7.4 us
    select_n x2, other arithmetic, shards(): jnp.where(inside[None, None, :], vectors[0], jnp.bfloat16(0))  7.04 us
    all_to_all x1, starting transfers between devices, shards(): lax.all_to_all(columns[0], 'group', split_axis=0, concat_axis=0, tiled=True)  3.72 us
    all_to_all x1, starting transfers between devices, shards(): lax.all_to_all(moved, 'group', split_axis=0, concat_axis=0, tiled=True)  3.6 us
  transfers between devices with their start and end apart: 12, of which 10 were waited for; matrix products, arithmetic and copies ran while one was open for 9% of the time, Pallas kernels for 0%

profile of v1, /device:TPU:0, one launch (start us, length us, event | category | flops | bytes accessed | tf_op | source)
XLA Modules:
  0.0 123.7 jit_solution(9892331393297519981)
XLA Ops:
  0.7 2.5 %bitcast_select_fusion = bf16[8,128,2048]{2,1,0:T(8,128)(2,1)S(1)} fusion(bf16[1,8,128,2048]{3,2,1,0:T(8,128)(2,1)} %param.7, pred[2048]{0:T(1024)(128)(4,1)S(1)} %add_compare_fusion), kind=kLoop, calls=%fused_computation | loop fusion | flops 2097152 | bytes 8390656 | tf_op jit(solution)/shard_map/jit(_where)/select_n | solution.py:39
  4.1 1.1 copy-done
  5.5 0.7 pad_maximum_fusion.1
  6.2 3.0 %collective-permute-start.2 = (f32[4,128,128]{2,1,0:T(8,128)}, f32[4,128,128]{2,1,0:T(8,128)S(1)}, u32[]{:S(2)}, u32[]{:S(2)}) collective-permute-start(f32[4,128,128]{2,1,0:T(8,128)} %pad_maximum_fusion.1), channel_id=1, source_target_pairs={{0,1},{1,0},{2,3},{3,2},{4,5},{5,4},{6,7},{7,6},{8,9},{9,8},{10,11... | collective-permute-start | bytes 786440 | tf_op jit(solution)/shard_map/ppermute | solution.py:16
  9.3 3.7 %all-to-all-start = ((f32[8,16,2048]{2,1,0:T(8,128)}), f32[8,16,2048]{2,1,0:T(8,128)S(1)}, u32[]{:S(2)}, u32[]{:S(2)}) async-start(f32[8,16,2048]{2,1,0:T(8,128)} %bitcast.1), calls=%async_computation | async-start | bytes 2097152 | tf_op jit(solution)/shard_map/all_to_all | solution.py:33
  13.0 4.6 %bitcast_select_fusion.1 = bf16[1024,2048]{1,0:T(8,128)(2,1)} fusion(bf16[1,8,128,2048]{3,2,1,0:T(8,128)(2,1)} %param.7, pred[2048]{0:T(1024)(128)(4,1)S(1)} %add_compare_fusion), kind=kLoop, calls=%fused_computation.1 | loop fusion | flops 2097152 | bytes 8390656 | tf_op jit(solution)/shard_map/jit(_where)/select_n | solution.py:39
  17.6 0.4 fusion.71
  18.8 0.8 slice-done
  19.6 1.6 %fusion.73 = f32[256,512]{1,0:T(8,128)} fusion(bf16[256,2048]{1,0:T(8,128)(2,1)S(1)} %bitcast.114, bf16[512,2048]{1,0:T(8,128)(2,1)S(1)} %bitcast.109), kind=kOutput, calls=%fused_computation.126 | convolution fusion | flops 536870912 | bytes 3670016 | tf_op jit(solution)/shard_map/dot_general | solution.py:27
  21.2 1.0 fusion.74
  22.3 0.8 slice_bitcast_fusion.19
  23.1 2.6 %collective-permute-start.3 = (f32[4,128,128]{2,1,0:T(8,128)S(1)}, f32[4,128,128]{2,1,0:T(8,128)S(1)}, u32[]{:S(2)}, u32[]{:S(2)}) collective-permute-start(f32[4,128,128]{2,1,0:T(8,128)S(1)} %fusion.70), channel_id=1, source_target_pairs={{0,2},{1,3},{2,0},{3,1},{4,6},{5,7},{6,4},{7,5},{8,10},{9,11},{10,... | collective-permute-start | bytes 786440 | tf_op jit(solution)/shard_map/ppermute | solution.py:16
  25.8 0.5 fusion.72
  26.3 12.0 %collective-permute-done.3 = f32[4,128,128]{2,1,0:T(8,128)S(1)} collective-permute-done((f32[4,128,128]{2,1,0:T(8,128)S(1)}, f32[4,128,128]{2,1,0:T(8,128)S(1)}, u32[]{:S(2)}, u32[]{:S(2)}) %collective-permute-start.3) | collective-permute-done | bytes 262176 | tf_op jit(solution)/shard_map/ppermute | solution.py:16
  38.6 3.5 %fusion.1 = f32[256,1024]{1,0:T(8,128)S(1)} fusion(bf16[1024,2048]{1,0:T(8,128)(2,1)} %bitcast_select_fusion.1, bf16[128,2048]{1,0:T(8,128)(2,1)S(1)} %get-tuple-element.10, bf16[128,2048]{1,0:T(8,128)(2,1)S(1)} %get-tuple-element.9), kind=kOutput, calls=%fused_computation.18 | convolution fusion | flops 1075838976 | bytes 6291456 | tf_op jit(solution)/shard_map/dot_general | solution.py:27
  42.5 5.2 %collective-permute-done = f32[128,256]{1,0:T(8,128)S(1)} collective-permute-done((f32[128,256]{1,0:T(8,128)S(1)}, f32[128,256]{1,0:T(8,128)S(1)}, u32[]{:S(2)}, u32[]{:S(2)}) %collective-permute-start) | collective-permute-done | bytes 131104 | tf_op jit(solution)/shard_map/ppermute | solution.py:16
  47.8 1.1 collective-permute-start.1
  49.0 7.1 %collective-permute-done.1 = f32[128,256]{1,0:T(8,128)S(1)} collective-permute-done((f32[128,256]{1,0:T(8,128)S(1)}, f32[128,256]{1,0:T(8,128)S(1)}, u32[]{:S(2)}, u32[]{:S(2)}) %collective-permute-start.1) | collective-permute-done | bytes 131104 | tf_op jit(solution)/shard_map/ppermute | solution.py:16
  56.1 0.4 fusion.21
  57.3 5.2 %collective-permute-done.4 = f32[128,256]{1,0:T(8,128)S(1)} collective-permute-done((f32[128,256]{1,0:T(8,128)S(1)}, f32[128,256]{1,0:T(8,128)S(1)}, u32[]{:S(2)}, u32[]{:S(2)}) %collective-permute-start.4) | collective-permute-done | bytes 131104 | tf_op jit(solution)/shard_map/ppermute | solution.py:16
  62.9 7.9 %collective-permute-done.5 = f32[128,256]{1,0:T(8,128)S(1)} collective-permute-done((f32[128,256]{1,0:T(8,128)S(1)}, f32[128,256]{1,0:T(8,128)S(1)}, u32[]{:S(2)}, u32[]{:S(2)}) %collective-permute-start.5) | collective-permute-done | bytes 131104 | tf_op jit(solution)/shard_map/ppermute | solution.py:16
  71.2 0.7 convolution_subtract_fusion
  72.2 5.2 %collective-permute-done.6 = f32[128,256]{1,0:T(8,128)S(1)} collective-permute-done((f32[128,256]{1,0:T(8,128)S(1)}, f32[128,256]{1,0:T(8,128)S(1)}, u32[]{:S(2)}, u32[]{:S(2)}) %collective-permute-start.6) | collective-permute-done | bytes 131104 | tf_op jit(solution)/shard_map/ppermute | solution.py:16
  77.7 8.0 %collective-permute-done.7 = f32[128,256]{1,0:T(8,128)S(1)} collective-permute-done((f32[128,256]{1,0:T(8,128)S(1)}, f32[128,256]{1,0:T(8,128)S(1)}, u32[]{:S(2)}, u32[]{:S(2)}) %collective-permute-start.7) | collective-permute-done | bytes 131104 | tf_op jit(solution)/shard_map/ppermute | solution.py:16
  86.1 0.9 convolution_subtract_fusion.2
  87.3 5.1 %collective-permute-done.8 = f32[128,256]{1,0:T(8,128)S(1)} collective-permute-done((f32[128,256]{1,0:T(8,128)S(1)}, f32[128,256]{1,0:T(8,128)S(1)}, u32[]{:S(2)}, u32[]{:S(2)}) %collective-permute-start.8) | collective-permute-done | bytes 131104 | tf_op jit(solution)/shard_map/ppermute | solution.py:16
  92.7 8.0 %collective-permute-done.9 = f32[128,256]{1,0:T(8,128)S(1)} collective-permute-done((f32[128,256]{1,0:T(8,128)S(1)}, f32[128,256]{1,0:T(8,128)S(1)}, u32[]{:S(2)}, u32[]{:S(2)}) %collective-permute-start.9) | collective-permute-done | bytes 131104 | tf_op jit(solution)/shard_map/ppermute | solution.py:16
  101.2 1.3 %fusion.6 = f32[256,2048]{1,0:T(8,128)S(1)} fusion(bf16[1024,2048]{1,0:T(8,128)(2,1)S(1)} %copy-done.2, bf16[128,1024]{1,0:T(8,128)(2,1)S(1)} %get-tuple-element.12, bf16[128,1024]{1,0:T(8,128)(2,1)S(1)} %get-tuple-element.11), kind=kOutput, calls=%fused_computation.36 | convolution fusion | flops 1074790400 | bytes 6815744 | tf_op jit(solution)/shard_map/dot_general | solution.py:27
  102.5 1.2 slice_subtract_fusion
  103.7 3.6 %all-to-all-start.1 = ((f32[8,16,2048]{2,1,0:T(8,128)}), f32[8,16,2048]{2,1,0:T(8,128)S(1)}, u32[]{:S(2)}, u32[]{:S(2)}) async-start(f32[8,16,2048]{2,1,0:T(8,128)} %bitcast.38), calls=%async_computation.1 | async-start | bytes 2097152 | tf_op jit(solution)/shard_map/all_to_all | solution.py:87
  107.3 15.3 %all-to-all-done.1 = f32[8,16,2048]{2,1,0:T(8,128)S(1)} async-done(((f32[8,16,2048]{2,1,0:T(8,128)}), f32[8,16,2048]{2,1,0:T(8,128)S(1)}, u32[]{:S(2)}, u32[]{:S(2)}) %all-to-all-start.1) | async-done | bytes 1048608 | tf_op jit(solution)/shard_map/all_to_all | solution.py:87
  122.6 1.1 select_bitcast_fusion
  (65 shorter events, 5.7 us)
Async XLA Ops:
  3.1 2.0 %copy-start = (bf16[8,128,2048]{2,1,0:T(8,128)(2,1)}, bf16[8,128,2048]{2,1,0:T(8,128)(2,1)S(1)}, u32[]{:S(2)}) copy-start(bf16[8,128,2048]{2,1,0:T(8,128)(2,1)S(1)} %bitcast_select_fusion) | copy-start | bytes 12582916
  6.2 16.9 %collective-permute-start.2 = (f32[4,128,128]{2,1,0:T(8,128)}, f32[4,128,128]{2,1,0:T(8,128)S(1)}, u32[]{:S(2)}, u32[]{:S(2)}) collective-permute-start(f32[4,128,128]{2,1,0:T(8,128)} %pad_maximum_fusion.1), channel_id=1, source_target_pairs={{0,1},{1,0},{2,3},{3,2},{4,5},{5,4},{6,7},{7,6},{8,9},{9,8},{10,11... | collective-permute-start | bytes 786440 | tf_op jit(solution)/shard_map/ppermute | solution.py:16
  9.3 29.1 %all-to-all-start = ((f32[8,16,2048]{2,1,0:T(8,128)}), f32[8,16,2048]{2,1,0:T(8,128)S(1)}, u32[]{:S(2)}, u32[]{:S(2)}) async-start(f32[8,16,2048]{2,1,0:T(8,128)} %bitcast.1), calls=%async_computation | async-start | bytes 2097152 | tf_op jit(solution)/shard_map/all_to_all | solution.py:33
  13.0 4.6 %copy-start.1 = (bf16[8,128,2048]{2,1,0:T(8,128)(2,1)S(1)}, bf16[8,128,2048]{2,1,0:T(8,128)(2,1)}, u32[]{:S(2)}) copy-start(bf16[8,128,2048]{2,1,0:T(8,128)(2,1)} %copy-done) | copy-start | bytes 12582916
  18.0 1.6 %slice-start = ((bf16[8,128,2048]{2,1,0:T(8,128)(2,1)}), bf16[4,128,2048]{2,1,0:T(8,128)(2,1)S(1)}, s32[]{:S(2)}) async-start(bf16[8,128,2048]{2,1,0:T(8,128)(2,1)} %copy-done), calls=%async_computation.2 | async-start | bytes 4194304 | tf_op jit(solution)/shard_map/slice | solution.py:78
  18.0 3.2 %slice-start.1 = ((bf16[8,128,2048]{2,1,0:T(8,128)(2,1)}), bf16[6,128,2048]{2,1,0:T(8,128)(2,1)S(1)}, s32[]{:S(2)}) async-start(bf16[8,128,2048]{2,1,0:T(8,128)(2,1)} %copy-done), calls=%async_computation.3 | async-start | bytes 6291456 | tf_op jit(solution)/shard_map/slice | solution.py:78
  19.6 2.6 %copy-start.4 = (f32[1,8,128,128]{3,2,1,0:T(8,128)S(1)}, f32[1,8,128,128]{3,2,1,0:T(8,128)}, u32[]{:S(2)}) copy-start(f32[1,8,128,128]{3,2,1,0:T(8,128)} %param.8) | copy-start | bytes 1572868
  23.1 15.2 %collective-permute-start.3 = (f32[4,128,128]{2,1,0:T(8,128)S(1)}, f32[4,128,128]{2,1,0:T(8,128)S(1)}, u32[]{:S(2)}, u32[]{:S(2)}) collective-permute-start(f32[4,128,128]{2,1,0:T(8,128)S(1)} %fusion.70), channel_id=1, source_target_pairs={{0,2},{1,3},{2,0},{3,1},{4,6},{5,7},{6,4},{7,5},{8,10},{9,11},{10,... | collective-permute-start | bytes 786440 | tf_op jit(solution)/shard_map/ppermute | solution.py:16
  38.5 17.6 %copy-start.9 = (f32[128,128]{1,0:T(8,128)S(1)}, f32[128,128]{1,0:T(8,128)}, u32[]{:S(2)}) copy-start(f32[128,128]{1,0:T(8,128)} %get-tuple-element.19) | copy-start | bytes 196612
  38.5 17.6 %copy-start.10 = (f32[128,128]{1,0:T(8,128)S(1)}, f32[128,128]{1,0:T(8,128)}, u32[]{:S(2)}) copy-start(f32[128,128]{1,0:T(8,128)} %get-tuple-element.20) | copy-start | bytes 196612
  38.5 32.3 %copy-start.7 = (f32[128,128]{1,0:T(8,128)S(1)}, f32[128,128]{1,0:T(8,128)}, u32[]{:S(2)}) copy-start(f32[128,128]{1,0:T(8,128)} %get-tuple-element.17) | copy-start | bytes 196612
  38.5 32.3 %copy-start.8 = (f32[128,128]{1,0:T(8,128)S(1)}, f32[128,128]{1,0:T(8,128)}, u32[]{:S(2)}) copy-start(f32[128,128]{1,0:T(8,128)} %get-tuple-element.18) | copy-start | bytes 196612
  42.1 29.1 %copy-start.3 = (f32[256,512]{1,0:T(8,128)S(1)}, f32[256,512]{1,0:T(8,128)}, u32[]{:S(2)}) copy-start(f32[256,512]{1,0:T(8,128)} %fusion.73) | copy-start | bytes 1572868
  42.1 43.6 %copy-start.5 = (f32[128,128]{1,0:T(8,128)S(1)}, f32[128,128]{1,0:T(8,128)}, u32[]{:S(2)}) copy-start(f32[128,128]{1,0:T(8,128)} %get-tuple-element.15) | copy-start | bytes 196612
  42.1 43.6 %copy-start.6 = (f32[128,128]{1,0:T(8,128)S(1)}, f32[128,128]{1,0:T(8,128)}, u32[]{:S(2)}) copy-start(f32[128,128]{1,0:T(8,128)} %get-tuple-element.16) | copy-start | bytes 196612
  42.2 5.5 %collective-permute-start = (f32[128,256]{1,0:T(8,128)S(1)}, f32[128,256]{1,0:T(8,128)S(1)}, u32[]{:S(2)}, u32[]{:S(2)}) collective-permute-start(f32[128,256]{1,0:T(8,128)S(1)} %slice.185), channel_id=1, source_target_pairs={{0,1},{1,0},{2,3},{3,2},{4,5},{5,4},{6,7},{7,6},{8,9},{9,8},{10,11... | collective-permute-start | bytes 393224 | tf_op jit(solution)/shard_map/ppermute | solution.py:16
  47.8 8.4 %collective-permute-start.1 = (f32[128,256]{1,0:T(8,128)S(1)}, f32[128,256]{1,0:T(8,128)S(1)}, u32[]{:S(2)}, u32[]{:S(2)}) collective-permute-start(f32[128,256]{1,0:T(8,128)S(1)} %slice_add_fusion.1), channel_id=1, source_target_pairs={{0,2},{1,3},{2,0},{3,1},{4,6},{5,7},{6,4},{7,5},{8,10},{9,11},{10,... | collective-permute-start | bytes 393224 | tf_op jit(solution)/shard_map/ppermute | solution.py:16
  56.6 44.6 %copy-start.2 = (bf16[1024,2048]{1,0:T(8,128)(2,1)S(1)}, bf16[1024,2048]{1,0:T(8,128)(2,1)}, u32[]{:S(2)}) copy-start(bf16[1024,2048]{1,0:T(8,128)(2,1)} %bitcast_select_fusion.1) | copy-start | bytes 12582916
  57.0 5.5 %collective-permute-start.4 = (f32[128,256]{1,0:T(8,128)S(1)}, f32[128,256]{1,0:T(8,128)S(1)}, u32[]{:S(2)}, u32[]{:S(2)}) collective-permute-start(f32[128,256]{1,0:T(8,128)S(1)} %convolution_subtract_fusion.1), channel_id=1, source_target_pairs={{0,1},{1,0},{2,3},{3,2},{4,5},{5,4},{6,7},{7,6},{8,9},{9,8},{10,11... | collective-permute-start | bytes 393224 | tf_op jit(solution)/shard_map/ppermute | solution.py:16
  62.5 8.3 %collective-permute-start.5 = (f32[128,256]{1,0:T(8,128)S(1)}, f32[128,256]{1,0:T(8,128)S(1)}, u32[]{:S(2)}, u32[]{:S(2)}) collective-permute-start(f32[128,256]{1,0:T(8,128)S(1)} %add.58), channel_id=1, source_target_pairs={{0,2},{1,3},{2,0},{3,1},{4,6},{5,7},{6,4},{7,5},{8,10},{9,11},{10,... | collective-permute-start | bytes 393224 | tf_op jit(solution)/shard_map/ppermute | solution.py:16
  71.9 5.4 %collective-permute-start.6 = (f32[128,256]{1,0:T(8,128)S(1)}, f32[128,256]{1,0:T(8,128)S(1)}, u32[]{:S(2)}, u32[]{:S(2)}) collective-permute-start(f32[128,256]{1,0:T(8,128)S(1)} %convolution_subtract_fusion), channel_id=1, source_target_pairs={{0,1},{1,0},{2,3},{3,2},{4,5},{5,4},{6,7},{7,6},{8,9},{9,8},{10,11... | collective-permute-start | bytes 393224 | tf_op jit(solution)/shard_map/ppermute | solution.py:16
  77.4 8.3 %collective-permute-start.7 = (f32[128,256]{1,0:T(8,128)S(1)}, f32[128,256]{1,0:T(8,128)S(1)}, u32[]{:S(2)}, u32[]{:S(2)}) collective-permute-start(f32[128,256]{1,0:T(8,128)S(1)} %add.60), channel_id=1, source_target_pairs={{0,2},{1,3},{2,0},{3,1},{4,6},{5,7},{6,4},{7,5},{8,10},{9,11},{10,... | collective-permute-start | bytes 393224 | tf_op jit(solution)/shard_map/ppermute | solution.py:16
  87.0 5.4 %collective-permute-start.8 = (f32[128,256]{1,0:T(8,128)S(1)}, f32[128,256]{1,0:T(8,128)S(1)}, u32[]{:S(2)}, u32[]{:S(2)}) collective-permute-start(f32[128,256]{1,0:T(8,128)S(1)} %convolution_subtract_fusion.2), channel_id=1, source_target_pairs={{0,1},{1,0},{2,3},{3,2},{4,5},{5,4},{6,7},{7,6},{8,9},{9,8},{10,11... | collective-permute-start | bytes 393224 | tf_op jit(solution)/shard_map/ppermute | solution.py:16
  92.4 8.3 %collective-permute-start.9 = (f32[128,256]{1,0:T(8,128)S(1)}, f32[128,256]{1,0:T(8,128)S(1)}, u32[]{:S(2)}, u32[]{:S(2)}) collective-permute-start(f32[128,256]{1,0:T(8,128)S(1)} %add.62), channel_id=1, source_target_pairs={{0,2},{1,3},{2,0},{3,1},{4,6},{5,7},{6,4},{7,5},{8,10},{9,11},{10,... | collective-permute-start | bytes 393224 | tf_op jit(solution)/shard_map/ppermute | solution.py:16
  102.5 4.8 %copy-start.11 = (s32[1,8]{1,0:T(1,128)S(1)}, s32[1,8]{1,0:T(1,128)}, u32[]{:S(2)}) copy-start(s32[1,8]{1,0:T(1,128)} %param.11) | copy-start | bytes 100
  103.7 19.0 %all-to-all-start.1 = ((f32[8,16,2048]{2,1,0:T(8,128)}), f32[8,16,2048]{2,1,0:T(8,128)S(1)}, u32[]{:S(2)}, u32[]{:S(2)}) async-start(f32[8,16,2048]{2,1,0:T(8,128)} %bitcast.38), calls=%async_computation.1 | async-start | bytes 2097152 | tf_op jit(solution)/shard_map/all_to_all | solution.py:87

commit v2 on v0

v2 whole, which is shorter than its diff:
```python
import functools

import jax
import jax.numpy as jnp
from jax import lax
from jax.experimental import pallas as pl
from jax.experimental.pallas import tpu as pltpu
from jax.sharding import PartitionSpec as P


HIGH = lax.Precision.HIGHEST
SMEM = pl.BlockSpec(memory_space=pltpu.SMEM)
VMEM = pl.BlockSpec(memory_space=pltpu.VMEM)
ROWS, INNER = ((1,), (1,)), ((1,), (0,))


def dot(left, right, dims, precision=None):
    return lax.dot_general(
        left, right, (dims, ((), ())), precision=precision, preferred_element_type=jnp.float32)


def split(value):
    upper = lax.reduce_precision(value, 8, 7)
    return jnp.concatenate([upper, value - upper], axis=0).astype(jnp.bfloat16)


def folded(value):
    size = value.shape[0] // 2
    return value[:size] + value[size:]


def exchange(value, axis, step):
    count = lax.axis_size(axis)
    return lax.ppermute(value, axis, [(i, i ^ step) for i in range(count)])


def total(value, axis):
    count = lax.axis_size(axis)
    if count & (count - 1):
        return lax.psum(value, axis)
    step = 1
    while step < count:
        value = value + exchange(value, axis, step)
        step *= 2
    return value


def halving_total(value, axis):
    count = lax.axis_size(axis)
    if count & (count - 1):
        return lax.psum(value, axis)
    me = lax.axis_index(axis)
    steps, step = [], 1
    while step < count:
        half = value.shape[0] // 2
        if value.shape[0] % 2 == 0:
            bit = (me // step) % 2
            keep = lax.dynamic_slice_in_dim(value, bit * half, half, 0)
            give = lax.dynamic_slice_in_dim(value, (1 - bit) * half, half, 0)
            value = keep + exchange(give, axis, step)
            steps.append((step, bit))
        else:
            value = value + exchange(value, axis, step)
        step *= 2
    for step, bit in reversed(steps):
        other = exchange(value, axis, step)
        first = jnp.where(bit == 0, value, other)
        second = jnp.where(bit == 0, other, value)
        value = jnp.concatenate([first, second], axis=0)
    return value


def partner(index, step, count):
    return index ^ step if count & (count - 1) == 0 else (step - index) % count


def reorder(sides, me_ref, held_ref, *outs):
    peers, slots, _ = held_ref.shape
    for number, side in enumerate(sides):
        panel_ref, parts_ref = outs[2 * number:2 * number + 2]
        size = len(side) * slots
        for index, step in enumerate(side):
            block = held_ref[partner(me_ref[0], step, peers)]
            upper = block.astype(jnp.bfloat16)
            panel_ref[index * slots:(index + 1) * slots, :] = block
            parts_ref[index * slots:(index + 1) * slots, :] = upper
            parts_ref[size + index * slots:size + (index + 1) * slots, :] = (
                block - upper.astype(jnp.float32)).astype(jnp.bfloat16)


def turn(blocks_ref, factors_ref, lower_ref, higher_ref):
    pairs = lower_ref.shape[0]
    for index in range(pairs):
        first = 2 * (pairs - 1 - index)
        for ref, block in ((lower_ref, first), (higher_ref, first + 1)):
            ref[index] = jnp.where(block < blocks_ref[0], factors_ref[block], 0.0).T


def place(me_ref, live_ref, *refs):
    *blocks, out = refs
    for step, block in enumerate(blocks):
        home = partner(me_ref[0], step, len(blocks))
        slot = lax.broadcasted_iota(jnp.int32, block.shape, 0)
        out[home] = jnp.where(slot < live_ref[home], block[...], 0.0)


def shards(columns, vectors, factors, order, blocks, live):
    count, width, rows = vectors.shape[1:]
    slots = columns.shape[2]
    peers = lax.axis_size("group")
    me = lax.axis_index("group").astype(jnp.int32)[None]
    quarter = peers // 4
    sides = [
        [*range(quarter), *range(peers - quarter, peers)],
        list(range(quarter, peers - quarter)),
    ]

    held = lax.all_to_all(columns[0], "group", split_axis=0, concat_axis=0, tiled=True)

    first_row = lax.axis_index("section") * rows
    inside = first_row + jnp.arange(rows) < order[0]
    basis = jnp.where(inside[None, :], vectors[0].reshape(count * width, rows), jnp.bfloat16(0))
    basis = lax.optimization_barrier(basis)
    tops = list(range(count, 0, -2))

    def span(low, high):
        return basis[low * width:high * width]

    piece = jax.ShapeDtypeStruct((count // 2, width, width), jnp.float32)
    lower, higher = pl.pallas_call(
        turn, out_shape=[piece, piece], in_specs=[SMEM, VMEM], out_specs=[VMEM] * 2, name="turn",
    )(blocks, factors[0])
    gram = jnp.stack([dot(span(top - 1, top), span(top - 2, top - 1), ROWS) for top in tops])
    gram = halving_total(gram, "section")
    crosses = [dot(span(top - 2, top), span(0, top - 2), ROWS) for top in tops[:-1]]
    batch = (((2,), (1,)), ((0,), (0,)))
    corner = -lax.dot_general(
        lax.dot_general(higher, gram, batch, precision=HIGH), lower, batch, precision=HIGH)
    merged = jnp.concatenate(
        [jnp.concatenate([lower, jnp.zeros_like(lower)], axis=2), jnp.concatenate([corner, higher], axis=2)],
        axis=1)

    outs = []
    for side in sides:
        size = len(side) * slots
        outs.append(jax.ShapeDtypeStruct((size, rows), jnp.float32))
        outs.append(jax.ShapeDtypeStruct((2 * size, rows), jnp.bfloat16))
    ordered = pl.pallas_call(
        functools.partial(reorder, sides),
        out_shape=outs, in_specs=[SMEM, VMEM], out_specs=[VMEM] * len(outs), name="reorder",
    )(me, held)

    returned = {}
    for number, side in enumerate(sides):
        panel, parts = ordered[2 * number:2 * number + 2]
        waiting = folded(dot(parts, basis, ROWS))
        known = []
        for index, top in enumerate(tops):
            inner = total(waiting[:, (top - 2) * width:], "section")
            weights = dot(inner, merged[index], INNER, HIGH)
            known.insert(0, weights)
            if top > 2:
                waiting = waiting[:, :(top - 2) * width] - dot(weights, crosses[index], INNER, HIGH)
        moved = panel - folded(dot(split(jnp.concatenate(known, axis=1)), basis, INNER))
        for index, step in enumerate(side):
            block = moved[index * slots:(index + 1) * slots]
            if step or peers & (peers - 1):
                pairs = [(i, partner(i, step, peers)) for i in range(peers)]
                block = lax.ppermute(block, "group", pairs)
            returned[step] = block

    return pl.pallas_call(
        place,
        out_shape=jax.ShapeDtypeStruct(columns.shape[1:], jnp.float32),
        in_specs=[SMEM, SMEM] + [VMEM] * peers, out_specs=VMEM, name="place",
    )(me, live[0], *[returned[step] for step in range(peers)])[None]


def solution(mesh):
    return jax.shard_map(
        shards,
        mesh=mesh,
        in_specs=(
            P("group", None, None, "section"),
            P("group", None, None, "section"),
            P("group", None, None, None),
            P("group"),
            P("group"),
            P("group", None),
        ),
        out_specs=P("group", None, None, "section"),
        check_vma=False,
    )
```

time: 234 us -> 115 us (0.49)
  waiting for transfers between devices: 152 us -> 30.1 us
  starting transfers between devices: 9.31 us -> 43.6 us
  matrix products: 45.1 us -> 24 us
  between operations: 14.7 us -> 1.88 us
  Pallas kernels: 0 us -> 7.07 us
  local copies, waits for them, and re-layouts: 6.94 us -> 3.47 us
    psum x4 -> x0, waiting for transfers between devices: 133 us -> none  [shards(): lax.psum(jnp.dot(transform_panel, joined.T, precision=high), 'section')]
    ppermute x0 -> x27, starting transfers between devices: none -> 39.9 us  [the longest x20 33.6 us: exchange(): return lax.ppermute(value, axis, [(i, i ^ step) for i in range(count)])]
    ppermute x0 -> x27, waiting for transfers between devices: none -> 30.1 us  [the longest x20 20.5 us: exchange(): return lax.ppermute(value, axis, [(i, i ^ step) for i in range(count)])]
    dot_general x21 -> x27, matrix products: 45.1 us -> 24 us  [the longest x25 21.3 us: dot(): lax.dot_general(left, right, (dims, ((), ())), precision=precision, prefe...]
    all_to_all x1 -> x0, waiting for transfers between devices: 15.3 us -> none  [shards(): lax.all_to_all(moved, 'group', split_axis=0, concat_axis=0, tiled=True)]
    pallas_call x0 -> x3, Pallas kernels: none -> 7.07 us  [the longest x1 2.65 us: shards(): pl.pallas_call(functools.partial(reorder, sides), out_shape=outs, in_spec...]
    mul x2 -> x0, other arithmetic: 4.52 us -> none  [the longest x1 3.37 us: shards(): basis_all = vectors[0].astype(jnp.float32) * inside[None, None, :]]
    all_to_all x1 -> x0, starting transfers between devices: 3.77 us -> none  [shards(): lax.all_to_all(moved, 'group', split_axis=0, concat_axis=0, tiled=True)]
  transfers between devices with their start and end apart: 6 -> 28, of which waited for: 6 -> 20; matrix products, arithmetic and copies ran while one was open for 7% -> 16% of each run, Pallas kernels for 0% -> 2%
where the time goes in v2:
time: 115 us; the launch traced here: 114 us
  starting transfers between devices  43.6 us (38%)
  waiting for transfers between devices  30.1 us (26%)
  matrix products  24 us (21%)
  Pallas kernels  7.07 us (6%)
  other arithmetic  4.07 us (4%)
  local copies, waits for them, and re-layouts  3.47 us (3%)
  between operations  1.88 us (2%)
    ppermute x20, starting transfers between devices, exchange(): return lax.ppermute(value, axis, [(i, i ^ step) for i in range(count)])  33.6 us
    dot_general x25, matrix products, dot(): lax.dot_general(left, right, (dims, ((), ())), precision=precision, prefe...  21.3 us
    ppermute x20, waiting for transfers between devices, exchange(): return lax.ppermute(value, axis, [(i, i ^ step) for i in range(count)])  20.5 us
    ppermute x7, waiting for transfers between devices, shards(): block = lax.ppermute(block, 'group', pairs)  9.6 us
    ppermute x7, starting transfers between devices, shards(): block = lax.ppermute(block, 'group', pairs)  6.29 us
    all_to_all x1, starting transfers between devices, shards(): lax.all_to_all(columns[0], 'group', split_axis=0, concat_axis=0, tiled=True)  3.73 us
    unnamed x28, local copies, waits for them, and re-layouts  2.69 us
    pallas_call x1, Pallas kernels, shards(): pl.pallas_call(functools.partial(reorder, sides), out_shape=outs, in_spec...  2.65 us
  transfers between devices with their start and end apart: 28, of which 20 were waited for; matrix products, arithmetic and copies ran while one was open for 16% of the time, Pallas kernels for 2%

profile of v2, /device:TPU:0, one launch (start us, length us, event | category | flops | bytes accessed | tf_op | source)
XLA Modules:
  0.0 114.2 jit_solution(10886329738523565910)
XLA Ops:
  0.7 2.5 %bitcast_select_fusion = bf16[1024,2048]{1,0:T(8,128)(2,1)S(1)} fusion(bf16[1,8,128,2048]{3,2,1,0:T(8,128)(2,1)} %param.7, pred[2048]{0:T(1024)(128)(4,1)S(1)} %add_compare_fusion), kind=kLoop, calls=%fused_computation | loop fusion | flops 2097152 | bytes 8390656 | tf_op jit(solution)/shard_map/jit(_where)/select_n | solution.py:122
  5.5 3.1 %collective-permute-start.2 = (f32[2,128,128]{2,1,0:T(8,128)S(1)}, f32[2,128,128]{2,1,0:T(8,128)S(1)}, u32[]{:S(2)}, u32[]{:S(2)}) collective-permute-start(f32[2,128,128]{2,1,0:T(8,128)S(1)} %constant_dynamic-slice_fusion.1), channel_id=1, source_target_pairs={{0,1},{1,0},{2,3},{3,2},{4,5},{5,4},{6,7},{7,6},{8,9},{9,8},{10,11... | collective-permute-start | bytes 393224 | tf_op jit(solution)/shard_map/ppermute | solution.py:34
  8.6 3.7 %all-to-all-start = ((f32[8,16,2048]{2,1,0:T(8,128)}), f32[8,16,2048]{2,1,0:T(8,128)S(1)}, u32[]{:S(2)}, u32[]{:S(2)}) async-start(f32[8,16,2048]{2,1,0:T(8,128)} %bitcast.2), calls=%async_computation | async-start | bytes 2097152 | tf_op jit(solution)/shard_map/all_to_all | solution.py:118
  12.4 2.6 %collective-permute-start.3 = (f32[1,128,128]{2,1,0:T(8,128)S(1)}, f32[1,128,128]{2,1,0:T(8,128)S(1)}, u32[]{:S(2)}, u32[]{:S(2)}) collective-permute-start(f32[1,128,128]{2,1,0:T(8,128)S(1)} %constant_dynamic-slice_fusion), channel_id=1, source_target_pairs={{0,2},{1,3},{2,0},{3,1},{4,6},{5,7},{6,4},{7,5},{8,10},{9,11},{10,... | collective-permute-start | bytes 196616 | tf_op jit(solution)/shard_map/ppermute | solution.py:34
  15.0 3.2 %fusion = f32[256,768]{1,0:T(8,128)S(1)} fusion(bf16[1024,2048]{1,0:T(8,128)(2,1)} %copy-done), kind=kOutput, calls=%fused_computation.1 | convolution fusion | flops 805306368 | bytes 4980736 | tf_op jit(solution)/shard_map/dot_general | solution.py:18
  19.1 1.5 %collective-permute-start.4 = (f32[1,128,128]{2,1,0:T(8,128)S(1)}, f32[1,128,128]{2,1,0:T(8,128)S(1)}, u32[]{:S(2)}, u32[]{:S(2)}) collective-permute-start(f32[1,128,128]{2,1,0:T(8,128)S(1)} %dynamic-slice_add_fusion.1), channel_id=1, source_target_pairs={{0,2},{1,3},{2,0},{3,1},{4,6},{5,7},{6,4},{7,5},{8,10},{9,11},{10,... | collective-permute-start | bytes 196616 | tf_op jit(solution)/shard_map/ppermute | solution.py:34
  20.6 2.7 %fusion.2 = f32[256,512]{1,0:T(8,128)S(1)} fusion(bf16[1024,2048]{1,0:T(8,128)(2,1)} %copy-done), kind=kOutput, calls=%fused_computation.3 | convolution fusion | flops 536870912 | bytes 3670016 | tf_op jit(solution)/shard_map/dot_general | solution.py:18
  23.3 1.8 %collective-permute-done.4 = f32[1,128,128]{2,1,0:T(8,128)S(1)} collective-permute-done((f32[1,128,128]{2,1,0:T(8,128)S(1)}, f32[1,128,128]{2,1,0:T(8,128)S(1)}, u32[]{:S(2)}, u32[]{:S(2)}) %collective-permute-start.4) | collective-permute-done | bytes 65568 | tf_op jit(solution)/shard_map/ppermute | solution.py:34
  25.4 2.7 %fusion.4 = f32[256,256]{1,0:T(8,128)} fusion(bf16[1024,2048]{1,0:T(8,128)(2,1)} %copy-done), kind=kOutput, calls=%fused_computation.16 | convolution fusion | flops 268435456 | bytes 2359296 | tf_op jit(solution)/shard_map/dot_general | solution.py:18
  28.8 2.0 %turn.1 = (f32[4,128,128]{2,1,0:T(8,128)}, f32[4,128,128]{2,1,0:T(8,128)}) custom-call(s32[1]{0:T(128)S(6)} %copy.12.blocks_ref, f32[8,128,128]{2,1,0:T(8,128)} %bitcast.54), custom_call_target="tpu_custom_call" | custom-call | tf_op jit(solution)/shard_map/turn/pallas_call | solution.py:130
  35.7 2.7 %reorder.1 = (f32[64,2048]{1,0:T(8,128)}, bf16[128,2048]{1,0:T(8,128)(2,1)}, f32[64,2048]{1,0:T(8,128)}, bf16[128,2048]{1,0:T(8,128)(2,1)}) custom-call(s32[1]{0:T(128)} %bitcast.me_ref, f32[8,16,2048]{2,1,0:T(8,128)} %copy-done.2), custom_call_target="tpu_custom_call" | custom-call | tf_op jit(solution)/shard_map/reorder/pallas_call | solution.py:148
  38.3 4.0 %fusion.55 = f32[128,1024]{1,0:T(8,128)S(1)} fusion(bf16[128,2048]{1,0:T(8,128)(2,1)} %get-tuple-element.16, bf16[1024,2048]{1,0:T(8,128)(2,1)} %copy-done), kind=kOutput, calls=%fused_computation.100 | convolution fusion | flops 536870912 | bytes 5242880 | tf_op jit(solution)/shard_map/dot_general | solution.py:18
  42.4 1.5 %fusion.54 = f32[128,1024]{1,0:T(8,128)S(1)} fusion(bf16[128,2048]{1,0:T(8,128)(2,1)S(1)} %copy-done.4, bf16[1024,2048]{1,0:T(8,128)(2,1)S(1)} %copy-done.1), kind=kOutput, calls=%fused_computation.99 | convolution fusion | flops 536870912 | bytes 5242880 | tf_op jit(solution)/shard_map/dot_general | solution.py:18
  44.0 1.8 %collective-permute-start.13 = (f32[64,256]{1,0:T(8,128)S(1)}, f32[64,256]{1,0:T(8,128)S(1)}, u32[]{:S(2)}, u32[]{:S(2)}) collective-permute-start(f32[64,256]{1,0:T(8,128)S(1)} %slice.221), channel_id=1, source_target_pairs={{0,1},{1,0},{2,3},{3,2},{4,5},{5,4},{6,7},{7,6},{8,9},{9,8},{10,11... | collective-permute-start | bytes 196616 | tf_op jit(solution)/shard_map/ppermute | solution.py:34
  46.2 2.1 %collective-permute-done.13 = f32[64,256]{1,0:T(8,128)S(1)} collective-permute-done((f32[64,256]{1,0:T(8,128)S(1)}, f32[64,256]{1,0:T(8,128)S(1)}, u32[]{:S(2)}, u32[]{:S(2)}) %collective-permute-start.13) | collective-permute-done | bytes 65568 | tf_op jit(solution)/shard_map/ppermute | solution.py:34
  48.3 3.2 %collective-permute-start.14 = (f32[64,256]{1,0:T(8,128)S(1)}, f32[64,256]{1,0:T(8,128)S(1)}, u32[]{:S(2)}, u32[]{:S(2)}) collective-permute-start(f32[64,256]{1,0:T(8,128)S(1)} %slice_add_fusion.6), channel_id=1, source_target_pairs={{0,2},{1,3},{2,0},{3,1},{4,6},{5,7},{6,4},{7,5},{8,10},{9,11},{10,... | collective-permute-start | bytes 196616 | tf_op jit(solution)/shard_map/ppermute | solution.py:34
  54.7 2.2 %collective-permute-start.15 = (f32[64,256]{1,0:T(8,128)S(1)}, f32[64,256]{1,0:T(8,128)S(1)}, u32[]{:S(2)}, u32[]{:S(2)}) collective-permute-start(f32[64,256]{1,0:T(8,128)S(1)} %slice.223), channel_id=1, source_target_pairs={{0,1},{1,0},{2,3},{3,2},{4,5},{5,4},{6,7},{7,6},{8,9},{9,8},{10,11... | collective-permute-start | bytes 196616 | tf_op jit(solution)/shard_map/ppermute | solution.py:34
  59.4 3.3 %collective-permute-start.16 = (f32[64,256]{1,0:T(8,128)S(1)}, f32[64,256]{1,0:T(8,128)S(1)}, u32[]{:S(2)}, u32[]{:S(2)}) collective-permute-start(f32[64,256]{1,0:T(8,128)S(1)} %slice_add_fusion.5), channel_id=1, source_target_pairs={{0,2},{1,3},{2,0},{3,1},{4,6},{5,7},{6,4},{7,5},{8,10},{9,11},{10,... | collective-permute-start | bytes 196616 | tf_op jit(solution)/shard_map/ppermute | solution.py:34
  62.7 1.9 %collective-permute-start.7 = (f32[64,256]{1,0:T(8,128)S(1)}, f32[64,256]{1,0:T(8,128)S(1)}, u32[]{:S(2)}, u32[]{:S(2)}) collective-permute-start(f32[64,256]{1,0:T(8,128)S(1)} %slice_add_fusion.8), channel_id=1, source_target_pairs={{0,2},{1,3},{2,0},{3,1},{4,6},{5,7},{6,4},{7,5},{8,10},{9,11},{10,... | collective-permute-start | bytes 196616 | tf_op jit(solution)/shard_map/ppermute | solution.py:34
  65.7 2.5 %collective-permute-start.17 = (f32[64,256]{1,0:T(8,128)S(1)}, f32[64,256]{1,0:T(8,128)S(1)}, u32[]{:S(2)}, u32[]{:S(2)}) collective-permute-start(f32[64,256]{1,0:T(8,128)S(1)} %slice.225), channel_id=1, source_target_pairs={{0,1},{1,0},{2,3},{3,2},{4,5},{5,4},{6,7},{7,6},{8,9},{9,8},{10,11... | collective-permute-start | bytes 196616 | tf_op jit(solution)/shard_map/ppermute | solution.py:34
  68.1 2.3 %collective-permute-done.7 = f32[64,256]{1,0:T(8,128)S(1)} collective-permute-done((f32[64,256]{1,0:T(8,128)S(1)}, f32[64,256]{1,0:T(8,128)S(1)}, u32[]{:S(2)}, u32[]{:S(2)}) %collective-permute-start.7) | collective-permute-done | bytes 65568 | tf_op jit(solution)/shard_map/ppermute | solution.py:34
  71.7 2.6 %collective-permute-start.18 = (f32[64,256]{1,0:T(8,128)S(1)}, f32[64,256]{1,0:T(8,128)S(1)}, u32[]{:S(2)}, u32[]{:S(2)}) collective-permute-start(f32[64,256]{1,0:T(8,128)S(1)} %slice_add_fusion.4), channel_id=1, source_target_pairs={{0,2},{1,3},{2,0},{3,1},{4,6},{5,7},{6,4},{7,5},{8,10},{9,11},{10,... | collective-permute-start | bytes 196616 | tf_op jit(solution)/shard_map/ppermute | solution.py:34
  77.4 2.4 %collective-permute-start.19 = (f32[64,256]{1,0:T(8,128)S(1)}, f32[64,256]{1,0:T(8,128)S(1)}, u32[]{:S(2)}, u32[]{:S(2)}) collective-permute-start(f32[64,256]{1,0:T(8,128)S(1)} %convolution_subtract_fusion.4), channel_id=1, source_target_pairs={{0,1},{1,0},{2,3},{3,2},{4,5},{5,4},{6,7},{7,6},{8,9},{9,8},{10,11... | collective-permute-start | bytes 196616 | tf_op jit(solution)/shard_map/ppermute | solution.py:34
  79.8 2.4 %collective-permute-done.9 = f32[64,256]{1,0:T(8,128)S(1)} collective-permute-done((f32[64,256]{1,0:T(8,128)S(1)}, f32[64,256]{1,0:T(8,128)S(1)}, u32[]{:S(2)}, u32[]{:S(2)}) %collective-permute-start.9) | collective-permute-done | bytes 65568 | tf_op jit(solution)/shard_map/ppermute | solution.py:34
  82.9 2.6 %collective-permute-start.20 = (f32[64,256]{1,0:T(8,128)S(1)}, f32[64,256]{1,0:T(8,128)S(1)}, u32[]{:S(2)}, u32[]{:S(2)}) collective-permute-start(f32[64,256]{1,0:T(8,128)S(1)} %add.127), channel_id=1, source_target_pairs={{0,2},{1,3},{2,0},{3,1},{4,6},{5,7},{6,4},{7,5},{8,10},{9,11},{10,... | collective-permute-start | bytes 196616 | tf_op jit(solution)/shard_map/ppermute | solution.py:34
  85.5 1.6 %collective-permute-done.10 = f32[64,256]{1,0:T(8,128)S(1)} collective-permute-done((f32[64,256]{1,0:T(8,128)S(1)}, f32[64,256]{1,0:T(8,128)S(1)}, u32[]{:S(2)}, u32[]{:S(2)}) %collective-permute-start.10) | collective-permute-done | bytes 65568 | tf_op jit(solution)/shard_map/ppermute | solution.py:34
  88.4 4.1 %collective-permute-done.11 = f32[64,256]{1,0:T(8,128)S(1)} collective-permute-done((f32[64,256]{1,0:T(8,128)S(1)}, f32[64,256]{1,0:T(8,128)S(1)}, u32[]{:S(2)}, u32[]{:S(2)}) %collective-permute-start.11) | collective-permute-done | bytes 65568 | tf_op jit(solution)/shard_map/ppermute | solution.py:34
  99.5 1.9 %collective-permute-start.25 = (f32[16,2048]{1,0:T(8,128)S(1)}, f32[16,2048]{1,0:T(8,128)S(1)}, u32[]{:S(2)}, u32[]{:S(2)}) collective-permute-start(f32[16,2048]{1,0:T(8,128)S(1)} %get-tuple-element.18), channel_id=1, source_target_pairs={{0,24},{4,28},{8,16},{12,20},{16,8},{20,12},{24,0},{28,4},{1,25},{... | collective-permute-start | bytes 393224 | tf_op jit(solution)/shard_map/ppermute | solution.py:169
  102.0 3.9 %collective-permute-done.21.refs_2_ = f32[16,2048]{1,0:T(8,128)S(1)} collective-permute-done((f32[16,2048]{1,0:T(8,128)S(1)}, f32[16,2048]{1,0:T(8,128)S(1)}, u32[]{:S(2)}, u32[]{:S(2)}) %collective-permute-start.21) | collective-permute-done | bytes 131104 | tf_op jit(solution)/shard_map/ppermute | solution.py:169
  105.9 1.5 %collective-permute-done.26.refs_7_ = f32[16,2048]{1,0:T(8,128)S(1)} collective-permute-done((f32[16,2048]{1,0:T(8,128)S(1)}, f32[16,2048]{1,0:T(8,128)S(1)}, u32[]{:S(2)}, u32[]{:S(2)}) %collective-permute-start.26) | collective-permute-done | bytes 131104 | tf_op jit(solution)/shard_map/ppermute | solution.py:169
  107.4 3.7 %collective-permute-done.25.refs_6_ = f32[16,2048]{1,0:T(8,128)S(1)} collective-permute-done((f32[16,2048]{1,0:T(8,128)S(1)}, f32[16,2048]{1,0:T(8,128)S(1)}, u32[]{:S(2)}, u32[]{:S(2)}) %collective-permute-start.25) | collective-permute-done | bytes 131104 | tf_op jit(solution)/shard_map/ppermute | solution.py:169
  111.8 2.4 %place.1 = f32[8,16,2048]{2,1,0:T(8,128)} custom-call(s32[1]{0:T(128)} %bitcast.me_ref, s32[8]{0:T(128)} %bitcast.55, f32[16,2048]{1,0:T(8,128)} %get-tuple-element.20.refs_0_, f32[16,2048]{1,0:T(8,128)} %copy-done.13, f32[16,2048]{1,0:T(8,128)} %copy-done.10, f32[16,2048]{1,0:T(8,128)} %copy-done.9, f32[16,2048]{1,0:T(8,128)} %copy-done.8, ...), custom_call_target="tpu_custom_call" | custom-call | tf_op jit(solution)/shard_map/place/pallas_call | solution.py:172
  (115 shorter events, 29.9 us)
Async XLA Ops:
  5.5 6.8 %collective-permute-start.2 = (f32[2,128,128]{2,1,0:T(8,128)S(1)}, f32[2,128,128]{2,1,0:T(8,128)S(1)}, u32[]{:S(2)}, u32[]{:S(2)}) collective-permute-start(f32[2,128,128]{2,1,0:T(8,128)S(1)} %constant_dynamic-slice_fusion.1), channel_id=1, source_target_pairs={{0,1},{1,0},{2,3},{3,2},{4,5},{5,4},{6,7},{7,6},{8,9},{9,8},{10,11... | collective-permute-start | bytes 393224 | tf_op jit(solution)/shard_map/ppermute | solution.py:34
  8.6 26.1 %all-to-all-start = ((f32[8,16,2048]{2,1,0:T(8,128)}), f32[8,16,2048]{2,1,0:T(8,128)S(1)}, u32[]{:S(2)}, u32[]{:S(2)}) async-start(f32[8,16,2048]{2,1,0:T(8,128)} %bitcast.2), calls=%async_computation | async-start | bytes 2097152 | tf_op jit(solution)/shard_map/all_to_all | solution.py:118
  12.4 6.7 %collective-permute-start.3 = (f32[1,128,128]{2,1,0:T(8,128)S(1)}, f32[1,128,128]{2,1,0:T(8,128)S(1)}, u32[]{:S(2)}, u32[]{:S(2)}) collective-permute-start(f32[1,128,128]{2,1,0:T(8,128)S(1)} %constant_dynamic-slice_fusion), channel_id=1, source_target_pairs={{0,2},{1,3},{2,0},{3,1},{4,6},{5,7},{6,4},{7,5},{8,10},{9,11},{10,... | collective-permute-start | bytes 196616 | tf_op jit(solution)/shard_map/ppermute | solution.py:34
  19.1 5.9 %collective-permute-start.4 = (f32[1,128,128]{2,1,0:T(8,128)S(1)}, f32[1,128,128]{2,1,0:T(8,128)S(1)}, u32[]{:S(2)}, u32[]{:S(2)}) collective-permute-start(f32[1,128,128]{2,1,0:T(8,128)S(1)} %dynamic-slice_add_fusion.1), channel_id=1, source_target_pairs={{0,2},{1,3},{2,0},{3,1},{4,6},{5,7},{6,4},{7,5},{8,10},{9,11},{10,... | collective-permute-start | bytes 196616 | tf_op jit(solution)/shard_map/ppermute | solution.py:34
  25.1 5.8 %collective-permute-start.5 = (f32[2,128,128]{2,1,0:T(8,128)S(1)}, f32[2,128,128]{2,1,0:T(8,128)S(1)}, u32[]{:S(2)}, u32[]{:S(2)}) collective-permute-start(f32[2,128,128]{2,1,0:T(8,128)S(1)} %pad_maximum_fusion.3), channel_id=1, source_target_pairs={{0,1},{1,0},{2,3},{3,2},{4,5},{5,4},{6,7},{7,6},{8,9},{9,8},{10,11... | collective-permute-start | bytes 393224 | tf_op jit(solution)/shard_map/ppermute | solution.py:34
  44.0 4.3 %collective-permute-start.13 = (f32[64,256]{1,0:T(8,128)S(1)}, f32[64,256]{1,0:T(8,128)S(1)}, u32[]{:S(2)}, u32[]{:S(2)}) collective-permute-start(f32[64,256]{1,0:T(8,128)S(1)} %slice.221), channel_id=1, source_target_pairs={{0,1},{1,0},{2,3},{3,2},{4,5},{5,4},{6,7},{7,6},{8,9},{9,8},{10,11... | collective-permute-start | bytes 196616 | tf_op jit(solution)/shard_map/ppermute | solution.py:34
  45.8 31.4 %copy-start.3 = (f32[256,256]{1,0:T(8,128)S(1)}, f32[256,256]{1,0:T(8,128)}, u32[]{:S(2)}) copy-start(f32[256,256]{1,0:T(8,128)} %fusion.4) | copy-start | bytes 786436
  45.8 5.6 %collective-permute-start = (f32[64,256]{1,0:T(8,128)S(1)}, f32[64,256]{1,0:T(8,128)S(1)}, u32[]{:S(2)}, u32[]{:S(2)}) collective-permute-start(f32[64,256]{1,0:T(8,128)S(1)} %slice.191), channel_id=1, source_target_pairs={{0,1},{1,0},{2,3},{3,2},{4,5},{5,4},{6,7},{7,6},{8,9},{9,8},{10,11... | collective-permute-start | bytes 196616 | tf_op jit(solution)/shard_map/ppermute | solution.py:34
  48.3 5.5 %collective-permute-start.14 = (f32[64,256]{1,0:T(8,128)S(1)}, f32[64,256]{1,0:T(8,128)S(1)}, u32[]{:S(2)}, u32[]{:S(2)}) collective-permute-start(f32[64,256]{1,0:T(8,128)S(1)} %slice_add_fusion.6), channel_id=1, source_target_pairs={{0,2},{1,3},{2,0},{3,1},{4,6},{5,7},{6,4},{7,5},{8,10},{9,11},{10,... | collective-permute-start | bytes 196616 | tf_op jit(solution)/shard_map/ppermute | solution.py:34
  51.5 5.7 %collective-permute-start.1 = (f32[64,256]{1,0:T(8,128)S(1)}, f32[64,256]{1,0:T(8,128)S(1)}, u32[]{:S(2)}, u32[]{:S(2)}) collective-permute-start(f32[64,256]{1,0:T(8,128)S(1)} %slice_add_fusion.9), channel_id=1, source_target_pairs={{0,2},{1,3},{2,0},{3,1},{4,6},{5,7},{6,4},{7,5},{8,10},{9,11},{10,... | collective-permute-start | bytes 196616 | tf_op jit(solution)/shard_map/ppermute | solution.py:34
  54.7 4.7 %collective-permute-start.15 = (f32[64,256]{1,0:T(8,128)S(1)}, f32[64,256]{1,0:T(8,128)S(1)}, u32[]{:S(2)}, u32[]{:S(2)}) collective-permute-start(f32[64,256]{1,0:T(8,128)S(1)} %slice.223), channel_id=1, source_target_pairs={{0,1},{1,0},{2,3},{3,2},{4,5},{5,4},{6,7},{7,6},{8,9},{9,8},{10,11... | collective-permute-start | bytes 196616 | tf_op jit(solution)/shard_map/ppermute | solution.py:34
  58.1 4.7 %collective-permute-start.6 = (f32[64,256]{1,0:T(8,128)S(1)}, f32[64,256]{1,0:T(8,128)S(1)}, u32[]{:S(2)}, u32[]{:S(2)}) collective-permute-start(f32[64,256]{1,0:T(8,128)S(1)} %slice.204), channel_id=1, source_target_pairs={{0,1},{1,0},{2,3},{3,2},{4,5},{5,4},{6,7},{7,6},{8,9},{9,8},{10,11... | collective-permute-start | bytes 196616 | tf_op jit(solution)/shard_map/ppermute | solution.py:34
  59.4 5.6 %collective-permute-start.16 = (f32[64,256]{1,0:T(8,128)S(1)}, f32[64,256]{1,0:T(8,128)S(1)}, u32[]{:S(2)}, u32[]{:S(2)}) collective-permute-start(f32[64,256]{1,0:T(8,128)S(1)} %slice_add_fusion.5), channel_id=1, source_target_pairs={{0,2},{1,3},{2,0},{3,1},{4,6},{5,7},{6,4},{7,5},{8,10},{9,11},{10,... | collective-permute-start | bytes 196616 | tf_op jit(solution)/shard_map/ppermute | solution.py:34
  62.7 7.7 %collective-permute-start.7 = (f32[64,256]{1,0:T(8,128)S(1)}, f32[64,256]{1,0:T(8,128)S(1)}, u32[]{:S(2)}, u32[]{:S(2)}) collective-permute-start(f32[64,256]{1,0:T(8,128)S(1)} %slice_add_fusion.8), channel_id=1, source_target_pairs={{0,2},{1,3},{2,0},{3,1},{4,6},{5,7},{6,4},{7,5},{8,10},{9,11},{10,... | collective-permute-start | bytes 196616 | tf_op jit(solution)/shard_map/ppermute | solution.py:34
  65.7 6.0 %collective-permute-start.17 = (f32[64,256]{1,0:T(8,128)S(1)}, f32[64,256]{1,0:T(8,128)S(1)}, u32[]{:S(2)}, u32[]{:S(2)}) collective-permute-start(f32[64,256]{1,0:T(8,128)S(1)} %slice.225), channel_id=1, source_target_pairs={{0,1},{1,0},{2,3},{3,2},{4,5},{5,4},{6,7},{7,6},{8,9},{9,8},{10,11... | collective-permute-start | bytes 196616 | tf_op jit(solution)/shard_map/ppermute | solution.py:34
  71.2 4.4 %collective-permute-start.8 = (f32[64,256]{1,0:T(8,128)S(1)}, f32[64,256]{1,0:T(8,128)S(1)}, u32[]{:S(2)}, u32[]{:S(2)}) collective-permute-start(f32[64,256]{1,0:T(8,128)S(1)} %slice.209), channel_id=1, source_target_pairs={{0,1},{1,0},{2,3},{3,2},{4,5},{5,4},{6,7},{7,6},{8,9},{9,8},{10,11... | collective-permute-start | bytes 196616 | tf_op jit(solution)/shard_map/ppermute | solution.py:34
  71.7 5.2 %collective-permute-start.18 = (f32[64,256]{1,0:T(8,128)S(1)}, f32[64,256]{1,0:T(8,128)S(1)}, u32[]{:S(2)}, u32[]{:S(2)}) collective-permute-start(f32[64,256]{1,0:T(8,128)S(1)} %slice_add_fusion.4), channel_id=1, source_target_pairs={{0,2},{1,3},{2,0},{3,1},{4,6},{5,7},{6,4},{7,5},{8,10},{9,11},{10,... | collective-permute-start | bytes 196616 | tf_op jit(solution)/shard_map/ppermute | solution.py:34
  75.6 6.6 %collective-permute-start.9 = (f32[64,256]{1,0:T(8,128)S(1)}, f32[64,256]{1,0:T(8,128)S(1)}, u32[]{:S(2)}, u32[]{:S(2)}) collective-permute-start(f32[64,256]{1,0:T(8,128)S(1)} %slice_add_fusion.7), channel_id=1, source_target_pairs={{0,2},{1,3},{2,0},{3,1},{4,6},{5,7},{6,4},{7,5},{8,10},{9,11},{10,... | collective-permute-start | bytes 196616 | tf_op jit(solution)/shard_map/ppermute | solution.py:34
  77.4 5.4 %collective-permute-start.19 = (f32[64,256]{1,0:T(8,128)S(1)}, f32[64,256]{1,0:T(8,128)S(1)}, u32[]{:S(2)}, u32[]{:S(2)}) collective-permute-start(f32[64,256]{1,0:T(8,128)S(1)} %convolution_subtract_fusion.4), channel_id=1, source_target_pairs={{0,1},{1,0},{2,3},{3,2},{4,5},{5,4},{6,7},{7,6},{8,9},{9,8},{10,11... | collective-permute-start | bytes 196616 | tf_op jit(solution)/shard_map/ppermute | solution.py:34
  82.5 11.0 %copy-start.6 = (f32[64,2048]{1,0:T(8,128)S(1)}, f32[64,2048]{1,0:T(8,128)}, u32[]{:S(2)}) copy-start(f32[64,2048]{1,0:T(8,128)} %get-tuple-element.15) | copy-start | bytes 1572868
  82.7 4.3 %collective-permute-start.10 = (f32[64,256]{1,0:T(8,128)S(1)}, f32[64,256]{1,0:T(8,128)S(1)}, u32[]{:S(2)}, u32[]{:S(2)}) collective-permute-start(f32[64,256]{1,0:T(8,128)S(1)} %convolution_subtract_fusion.5), channel_id=1, source_target_pairs={{0,1},{1,0},{2,3},{3,2},{4,5},{5,4},{6,7},{7,6},{8,9},{9,8},{10,11... | collective-permute-start | bytes 196616 | tf_op jit(solution)/shard_map/ppermute | solution.py:34
  82.9 5.2 %collective-permute-start.20 = (f32[64,256]{1,0:T(8,128)S(1)}, f32[64,256]{1,0:T(8,128)S(1)}, u32[]{:S(2)}, u32[]{:S(2)}) collective-permute-start(f32[64,256]{1,0:T(8,128)S(1)} %add.127), channel_id=1, source_target_pairs={{0,2},{1,3},{2,0},{3,1},{4,6},{5,7},{6,4},{7,5},{8,10},{9,11},{10,... | collective-permute-start | bytes 196616 | tf_op jit(solution)/shard_map/ppermute | solution.py:34
  87.1 5.4 %collective-permute-start.11 = (f32[64,256]{1,0:T(8,128)S(1)}, f32[64,256]{1,0:T(8,128)S(1)}, u32[]{:S(2)}, u32[]{:S(2)}) collective-permute-start(f32[64,256]{1,0:T(8,128)S(1)} %add.117), channel_id=1, source_target_pairs={{0,2},{1,3},{2,0},{3,1},{4,6},{5,7},{6,4},{7,5},{8,10},{9,11},{10,... | collective-permute-start | bytes 196616 | tf_op jit(solution)/shard_map/ppermute | solution.py:34
  93.7 5.9 %collective-permute-start.24 = (f32[16,2048]{1,0:T(8,128)S(1)}, f32[16,2048]{1,0:T(8,128)S(1)}, u32[]{:S(2)}, u32[]{:S(2)}) collective-permute-start(f32[16,2048]{1,0:T(8,128)S(1)} %get-tuple-element.21), channel_id=1, source_target_pairs={{0,20},{4,16},{8,28},{12,24},{16,4},{20,0},{24,12},{28,8},{1,21},{... | collective-permute-start | bytes 393224 | tf_op jit(solution)/shard_map/ppermute | solution.py:169
  93.7 8.1 %collective-permute-start.23 = (f32[16,2048]{1,0:T(8,128)S(1)}, f32[16,2048]{1,0:T(8,128)S(1)}, u32[]{:S(2)}, u32[]{:S(2)}) collective-permute-start(f32[16,2048]{1,0:T(8,128)S(1)} %get-tuple-element.22), channel_id=1, source_target_pairs={{0,16},{4,20},{8,24},{12,28},{16,0},{20,4},{24,8},{28,12},{1,17},{... | collective-permute-start | bytes 393224 | tf_op jit(solution)/shard_map/ppermute | solution.py:169
  96.5 5.4 %collective-permute-start.22 = (f32[16,2048]{1,0:T(8,128)S(1)}, f32[16,2048]{1,0:T(8,128)S(1)}, u32[]{:S(2)}, u32[]{:S(2)}) collective-permute-start(f32[16,2048]{1,0:T(8,128)S(1)} %get-tuple-element.23), channel_id=1, source_target_pairs={{0,12},{4,8},{8,4},{12,0},{16,28},{20,24},{24,20},{28,16},{1,13},{... | collective-permute-start | bytes 393224 | tf_op jit(solution)/shard_map/ppermute | solution.py:169
  97.9 8.0 %collective-permute-start.21 = (f32[16,2048]{1,0:T(8,128)S(1)}, f32[16,2048]{1,0:T(8,128)S(1)}, u32[]{:S(2)}, u32[]{:S(2)}) collective-permute-start(f32[16,2048]{1,0:T(8,128)S(1)} %get-tuple-element.24), channel_id=1, source_target_pairs={{0,8},{4,12},{8,0},{12,4},{16,24},{20,28},{24,16},{28,20},{1,9},{5... | collective-permute-start | bytes 393224 | tf_op jit(solution)/shard_map/ppermute | solution.py:169
  98.7 8.7 %collective-permute-start.26 = (f32[16,2048]{1,0:T(8,128)S(1)}, f32[16,2048]{1,0:T(8,128)S(1)}, u32[]{:S(2)}, u32[]{:S(2)}) collective-permute-start(f32[16,2048]{1,0:T(8,128)S(1)} %get-tuple-element.17), channel_id=1, source_target_pairs={{0,28},{4,24},{8,20},{12,16},{16,12},{20,8},{24,4},{28,0},{1,29},{... | collective-permute-start | bytes 393224 | tf_op jit(solution)/shard_map/ppermute | solution.py:169
  99.5 11.6 %copy-start.7 = (f32[16,2048]{1,0:T(8,128)}, f32[16,2048]{1,0:T(8,128)S(1)}, u32[]{:S(2)}) copy-start(f32[16,2048]{1,0:T(8,128)S(1)} %collective-permute-done.24.refs_5_) | copy-start | bytes 393220
  99.5 11.6 %collective-permute-start.25 = (f32[16,2048]{1,0:T(8,128)S(1)}, f32[16,2048]{1,0:T(8,128)S(1)}, u32[]{:S(2)}, u32[]{:S(2)}) collective-permute-start(f32[16,2048]{1,0:T(8,128)S(1)} %get-tuple-element.18), channel_id=1, source_target_pairs={{0,24},{4,28},{8,16},{12,20},{16,8},{20,12},{24,0},{28,4},{1,25},{... | collective-permute-start | bytes 393224 | tf_op jit(solution)/shard_map/ppermute | solution.py:169
  101.8 9.3 %copy-start.8 = (f32[16,2048]{1,0:T(8,128)}, f32[16,2048]{1,0:T(8,128)S(1)}, u32[]{:S(2)}) copy-start(f32[16,2048]{1,0:T(8,128)S(1)} %collective-permute-done.23.refs_4_) | copy-start | bytes 393220
  101.8 9.3 %collective-permute-start.12 = (f32[16,2048]{1,0:T(8,128)S(1)}, f32[16,2048]{1,0:T(8,128)S(1)}, u32[]{:S(2)}, u32[]{:S(2)}) collective-permute-start(f32[16,2048]{1,0:T(8,128)S(1)} %get-tuple-element.19), channel_id=1, source_target_pairs={{0,4},{4,0},{8,12},{12,8},{16,20},{20,16},{24,28},{28,24},{1,5},{5... | collective-permute-start | bytes 393224 | tf_op jit(solution)/shard_map/ppermute | solution.py:169
  (10 other events, 32.8 us)

commit v3 on v0

v3 whole, which is shorter than its diff:
```python
import jax
import jax.numpy as jnp
from jax import lax
from jax.experimental import pallas as pl
from jax.experimental.pallas import tpu as pltpu
from jax.sharding import PartitionSpec as P


HIGH = lax.Precision.HIGHEST
SMEM = pl.BlockSpec(memory_space=pltpu.SMEM)
VMEM = pl.BlockSpec(memory_space=pltpu.VMEM)
ROWS, INNER = ((1,), (1,)), ((1,), (0,))


def dot(left, right, dims, precision=None):
    return lax.dot_general(
        left, right, (dims, ((), ())), precision=precision, preferred_element_type=jnp.float32)


def split(value):
    upper = lax.reduce_precision(value, 8, 7)
    return jnp.concatenate([upper, value - upper], axis=0).astype(jnp.bfloat16)


def folded(value):
    size = value.shape[0] // 2
    return value[:size] + value[size:]


def exchange(value, axis, step):
    count = lax.axis_size(axis)
    return lax.ppermute(value, axis, [(i, i ^ step) for i in range(count)])


def total(value, axis):
    count = lax.axis_size(axis)
    if count & (count - 1):
        return lax.psum(value, axis)
    step = 1
    while step < count:
        value = value + exchange(value, axis, step)
        step *= 2
    return value


def turn(blocks_ref, factors_ref, *outs):
    pairs = factors_ref.shape[0] // 2
    for index in range(pairs):
        first = 2 * (pairs - 1 - index)
        for ref, block in zip(outs[2 * min(index, 1):], (first, first + 1)):
            ref[max(index - 1, 0)] = jnp.where(block < blocks_ref[0], factors_ref[block], 0.0).T


def shards(columns, vectors, factors, order, blocks, live):
    count, width, rows = vectors.shape[1:]
    slots = columns.shape[2]
    pairs = count // 2
    turns = list(reversed(range(pairs)))

    held = lax.all_to_all(columns[0], "group", split_axis=0, concat_axis=0, tiled=True)

    inside = lax.axis_index("section") * rows + jnp.arange(rows) < order[0]
    basis = jnp.where(inside[None, :], vectors[0].reshape(count * width, rows), jnp.bfloat16(0))
    basis = lax.optimization_barrier(basis)

    def span(low, high):
        return basis[low * width:high * width]

    def product(pair):
        return dot(span(2 * pair + 1, 2 * pair + 2), span(2 * pair, 2 * pair + 1), ROWS)

    gram_first = total(product(turns[0])[None], "section")
    rest = jnp.stack([product(pair) for pair in turns[1:]])
    gram_rest = total(rest, "section")
    outs = [jax.ShapeDtypeStruct((size, width, width), jnp.float32) for size in (1, 1, pairs - 1, pairs - 1)]
    turned = pl.pallas_call(
        turn, out_shape=outs, in_specs=[SMEM, VMEM], out_specs=[VMEM] * 4, name="turn",
    )(blocks, factors[0])

    def merge(gram, lower, higher):
        batch = (((2,), (1,)), ((0,), (0,)))
        corner = -lax.dot_general(
            lax.dot_general(higher, gram, batch, precision=HIGH), lower, batch, precision=HIGH)
        return jnp.concatenate([
            jnp.concatenate([lower, jnp.zeros_like(lower)], axis=2),
            jnp.concatenate([corner, higher], axis=2)], axis=1)

    merged = [merge(gram_first, *turned[:2])[0]]
    rest = merge(gram_rest, *turned[2:])
    merged += [rest[index] for index in range(pairs - 1)]

    half = held.shape[0] // 2
    panels = [held[number * half:(number + 1) * half].reshape(half * slots, rows) for number in range(2)]
    for index, pair in enumerate(turns):
        vectors_of = span(2 * pair, 2 * pair + 2)
        for number, panel in enumerate(panels):
            inner = folded(dot(split(panel), vectors_of, ROWS))
            inner = total(inner, "section")
            weights = dot(inner, merged[index], INNER, HIGH)
            panels[number] = panel - folded(dot(split(weights), vectors_of, INNER))
    moved = [panel.reshape(half, slots, rows) for panel in panels]

    returned = lax.all_to_all(
        jnp.concatenate(moved, axis=0), "group", split_axis=0, concat_axis=0, tiled=True)
    keep = jnp.arange(slots)[None, :] < live[0][:, None]
    return jnp.where(keep[:, :, None], returned, jnp.float32(0.0))[None]


def solution(mesh):
    return jax.shard_map(
        shards,
        mesh=mesh,
        in_specs=(
            P("group", None, None, "section"),
            P("group", None, None, "section"),
            P("group", None, None, None),
            P("group"),
            P("group"),
            P("group", None),
        ),
        out_specs=P("group", None, None, "section"),
        check_vma=False,
    )
```

time: 234 us -> 107 us (0.46)
  waiting for transfers between devices: 152 us -> 39.9 us
  matrix products: 45.1 us -> 14.2 us
  starting transfers between devices: 9.31 us -> 39.4 us
  between operations: 14.7 us -> 1.86 us
  local copies, waits for them, and re-layouts: 6.94 us -> 2.02 us
    psum x4 -> x0, waiting for transfers between devices: 133 us -> none  [shards(): lax.psum(jnp.dot(transform_panel, joined.T, precision=high), 'section')]
    ppermute x0 -> x20, starting transfers between devices: none -> 32 us  [exchange(): return lax.ppermute(value, axis, [(i, i ^ step) for i in range(count)])]
    dot_general x21 -> x32, matrix products: 45.1 us -> 14.2 us  [the longest x28 9.57 us: dot(): lax.dot_general(left, right, (dims, ((), ())), precision=precision, prefe...]
    ppermute x0 -> x20, waiting for transfers between devices: none -> 24.6 us  [exchange(): return lax.ppermute(value, axis, [(i, i ^ step) for i in range(count)])]
    mul x2 -> x0, other arithmetic: 4.52 us -> none  [the longest x1 3.37 us: shards(): basis_all = vectors[0].astype(jnp.float32) * inside[None, None, :]]
    all_to_all x1, waiting for transfers between devices: 3.61 us -> 0.01 us  [shards(): lax.all_to_all(columns[0], 'group', split_axis=0, concat_axis=0, tiled=True)]
    squeeze x2 -> x0, local copies, waits for them, and re-layouts: 3.2 us -> none  [the longest x1 2.46 us: shards(): basis_all[2 * pair]]
    select_n x0 -> x1, other arithmetic: none -> 2.47 us  [shards(): jnp.where(inside[None, :], vectors[0].reshape(count * width, rows), jnp.b...]
  transfers between devices with their start and end apart: 6 -> 22, of which waited for: 6 -> 16; matrix products, arithmetic and copies ran while one was open for 7% -> 14% of each run, Pallas kernels for 0% -> 2%
where the time goes in v3:
time: 107 us
  waiting for transfers between devices  39.9 us (37%)
  starting transfers between devices  39.4 us (37%)
  matrix products  14.2 us (13%)
  other arithmetic  7.18 us (7%)
  local copies, waits for them, and re-layouts  2.02 us (2%)
  Pallas kernels  1.99 us (2%)
  between operations  1.86 us (2%)
    ppermute x20, starting transfers between devices, exchange(): return lax.ppermute(value, axis, [(i, i ^ step) for i in range(count)])  32 us
    ppermute x20, waiting for transfers between devices, exchange(): return lax.ppermute(value, axis, [(i, i ^ step) for i in range(count)])  24.6 us
    all_to_all x1, waiting for transfers between devices, shards(): lax.all_to_all(jnp.concatenate(moved, axis=0), 'group', split_axis=0, con...  15.3 us
    dot_general x28, matrix products, dot(): lax.dot_general(left, right, (dims, ((), ())), precision=precision, prefe...  9.57 us
    all_to_all x1, starting transfers between devices, shards(): lax.all_to_all(columns[0], 'group', split_axis=0, concat_axis=0, tiled=True)  3.72 us
    all_to_all x1, starting transfers between devices, shards(): lax.all_to_all(jnp.concatenate(moved, axis=0), 'group', split_axis=0, con...  3.67 us
    select_n x1, other arithmetic, shards(): jnp.where(inside[None, :], vectors[0].reshape(count * width, rows), jnp.b...  2.47 us
    dot_general x2, matrix products, merge(): lax.dot_general(higher, gram, batch, precision=HIGH)  2.31 us
  transfers between devices with their start and end apart: 22, of which 16 were waited for; matrix products, arithmetic and copies ran while one was open for 14% of the time, Pallas kernels for 2%

profile of v3, /device:TPU:0, one launch (start us, length us, event | category | flops | bytes accessed | tf_op | source)
XLA Modules:
  0.0 106.6 jit_solution(15353643434529769119)
XLA Ops:
  0.7 2.5 %bitcast_select_fusion = bf16[1024,2048]{1,0:T(8,128)(2,1)S(1)} fusion(bf16[1,8,128,2048]{3,2,1,0:T(8,128)(2,1)} %param.7, pred[2048]{0:T(1024)(128)(4,1)S(1)} %add_compare_fusion), kind=kLoop, calls=%fused_computation | loop fusion | flops 2097152 | bytes 8390656 | tf_op jit(solution)/shard_map/jit(_where)/select_n | solution.py:63
  4.1 3.1 %collective-permute-start.6 = (f32[3,128,128]{2,1,0:T(8,128)S(1)}, f32[3,128,128]{2,1,0:T(8,128)S(1)}, u32[]{:S(2)}, u32[]{:S(2)}) collective-permute-start(f32[3,128,128]{2,1,0:T(8,128)S(1)} %pad_maximum_fusion.1), channel_id=1, source_target_pairs={{0,1},{1,0},{2,3},{3,2},{4,5},{5,4},{6,7},{7,6},{8,9},{9,8},{10,11... | collective-permute-start | bytes 589832 | tf_op jit(solution)/shard_map/ppermute | solution.py:32
  8.5 3.7 %all-to-all-start = ((f32[8,16,2048]{2,1,0:T(8,128)}), f32[8,16,2048]{2,1,0:T(8,128)S(1)}, u32[]{:S(2)}, u32[]{:S(2)}) async-start(f32[8,16,2048]{2,1,0:T(8,128)} %bitcast.1), calls=%async_computation | async-start | bytes 2097152 | tf_op jit(solution)/shard_map/all_to_all | solution.py:60
  12.9 2.0 %turn.1 = (f32[1,128,128]{2,1,0:T(8,128)}, f32[1,128,128]{2,1,0:T(8,128)}, f32[3,128,128]{2,1,0:T(8,128)}, f32[3,128,128]{2,1,0:T(8,128)}) custom-call(s32[1]{0:T(128)S(6)} %copy.14.blocks_ref, f32[8,128,128]{2,1,0:T(8,128)} %bitcast.78), custom_call_target="tpu_custom_call" | custom-call | tf_op jit(solution)/shard_map/turn/pallas_call | solution.py:76
  14.9 2.7 %collective-permute-start.3 = (f32[1,128,128]{2,1,0:T(8,128)S(1)}, f32[1,128,128]{2,1,0:T(8,128)S(1)}, u32[]{:S(2)}, u32[]{:S(2)}) collective-permute-start(f32[1,128,128]{2,1,0:T(8,128)S(1)} %add.127), channel_id=1, source_target_pairs={{0,2},{1,3},{2,0},{3,1},{4,6},{5,7},{6,4},{7,5},{8,10},{9,11},{10,... | collective-permute-start | bytes 196616 | tf_op jit(solution)/shard_map/ppermute | solution.py:32
  18.0 8.4 %collective-permute-done.3 = f32[1,128,128]{2,1,0:T(8,128)S(1)} collective-permute-done((f32[1,128,128]{2,1,0:T(8,128)S(1)}, f32[1,128,128]{2,1,0:T(8,128)S(1)}, u32[]{:S(2)}, u32[]{:S(2)}) %collective-permute-start.3) | collective-permute-done | bytes 65568 | tf_op jit(solution)/shard_map/ppermute | solution.py:32
  26.4 1.0 fusion.131
  28.5 1.7 %collective-permute-done.7 = f32[3,128,128]{2,1,0:T(8,128)S(1)} collective-permute-done((f32[3,128,128]{2,1,0:T(8,128)S(1)}, f32[3,128,128]{2,1,0:T(8,128)S(1)}, u32[]{:S(2)}, u32[]{:S(2)}) %collective-permute-start.7) | collective-permute-done | bytes 196640 | tf_op jit(solution)/shard_map/ppermute | solution.py:32
  30.2 1.3 %fusion.88 = f32[3,128,128]{2,1,0:T(8,128)S(1)} fusion(f32[3,128,128]{2,1,0:T(8,128)} %get-tuple-element.12, f32[3,128,128]{2,1,0:T(8,128)S(1)} %fusion.165, f32[3,128,128]{2,1,0:T(8,128)S(1)} %collective-permute-done.7), kind=kOutput, calls=%fused_computation.129 | convolution fusion | flops 75546624 | bytes 786432 | tf_op jit(solution)/shard_map/dot_general | solution.py:83
  31.5 1.3 %convolution_negate_fusion = f32[3,128,128]{2,1,0:T(8,128)S(1)} fusion(f32[3,128,128]{2,1,0:T(8,128)S(1)} %fusion.88, f32[3,128,128]{2,1,0:T(8,128)} %get-tuple-element.11), kind=kOutput, calls=%fused_computation.1 | convolution fusion | flops 75546624 | bytes 589824 | tf_op jit(solution)/shard_map/dot_general | solution.py:82
  32.8 1.1 %select_maximum_fusion = f32[3,256,256]{2,1,0:T(8,128)S(1)} fusion(f32[3,128,128]{2,1,0:T(8,128)} %get-tuple-element.11, f32[3,128,128]{2,1,0:T(8,128)} %get-tuple-element.12, f32[3,128,128]{2,1,0:T(8,128)S(1)} %convolution_negate_fusion), kind=kLoop, calls=%fused_computation.10 | loop fusion | flops 786432 | bytes 1376256 | tf_op jit(solution)/shard_map/concatenate | solution.py:84
  34.1 1.9 %copy-done.1 = bf16[1024,2048]{1,0:T(8,128)(2,1)S(1)} copy-done((bf16[1024,2048]{1,0:T(8,128)(2,1)S(1)}, bf16[1024,2048]{1,0:T(8,128)(2,1)}, u32[]{:S(2)}) %copy-start.1) | copy-done | bytes 4194328
  37.4 1.8 %collective-permute-start = (f32[64,256]{1,0:T(8,128)S(1)}, f32[64,256]{1,0:T(8,128)S(1)}, u32[]{:S(2)}, u32[]{:S(2)}) collective-permute-start(f32[64,256]{1,0:T(8,128)S(1)} %slice_add_fusion.15), channel_id=1, source_target_pairs={{0,1},{1,0},{2,3},{3,2},{4,5},{5,4},{6,7},{7,6},{8,9},{9,8},{10,11... | collective-permute-start | bytes 196616 | tf_op jit(solution)/shard_map/ppermute | solution.py:32
  39.2 1.8 %collective-permute-done.12 = f32[64,256]{1,0:T(8,128)S(1)} collective-permute-done((f32[64,256]{1,0:T(8,128)S(1)}, f32[64,256]{1,0:T(8,128)S(1)}, u32[]{:S(2)}, u32[]{:S(2)}) %collective-permute-start.12) | collective-permute-done | bytes 65568 | tf_op jit(solution)/shard_map/ppermute | solution.py:32
  41.1 1.6 %collective-permute-start.13 = (f32[64,256]{1,0:T(8,128)S(1)}, f32[64,256]{1,0:T(8,128)S(1)}, u32[]{:S(2)}, u32[]{:S(2)}) collective-permute-start(f32[64,256]{1,0:T(8,128)S(1)} %fusion.184), channel_id=1, source_target_pairs={{0,2},{1,3},{2,0},{3,1},{4,6},{5,7},{6,4},{7,5},{8,10},{9,11},{10,... | collective-permute-start | bytes 196616 | tf_op jit(solution)/shard_map/ppermute | solution.py:32
  42.6 2.9 %collective-permute-start.1 = (f32[64,256]{1,0:T(8,128)S(1)}, f32[64,256]{1,0:T(8,128)S(1)}, u32[]{:S(2)}, u32[]{:S(2)}) collective-permute-start(f32[64,256]{1,0:T(8,128)S(1)} %fusion.180), channel_id=1, source_target_pairs={{0,2},{1,3},{2,0},{3,1},{4,6},{5,7},{6,4},{7,5},{8,10},{9,11},{10,... | collective-permute-start | bytes 196616 | tf_op jit(solution)/shard_map/ppermute | solution.py:32
  45.5 2.2 %collective-permute-done.13 = f32[64,256]{1,0:T(8,128)S(1)} collective-permute-done((f32[64,256]{1,0:T(8,128)S(1)}, f32[64,256]{1,0:T(8,128)S(1)}, u32[]{:S(2)}, u32[]{:S(2)}) %collective-permute-start.13) | collective-permute-done | bytes 65568 | tf_op jit(solution)/shard_map/ppermute | solution.py:32
  50.3 2.1 %collective-permute-start.4 = (f32[64,256]{1,0:T(8,128)S(1)}, f32[64,256]{1,0:T(8,128)S(1)}, u32[]{:S(2)}, u32[]{:S(2)}) collective-permute-start(f32[64,256]{1,0:T(8,128)S(1)} %slice_add_fusion.14), channel_id=1, source_target_pairs={{0,1},{1,0},{2,3},{3,2},{4,5},{5,4},{6,7},{7,6},{8,9},{9,8},{10,11... | collective-permute-start | bytes 196616 | tf_op jit(solution)/shard_map/ppermute | solution.py:32
  52.4 1.5 %collective-permute-done.14 = f32[64,256]{1,0:T(8,128)S(1)} collective-permute-done((f32[64,256]{1,0:T(8,128)S(1)}, f32[64,256]{1,0:T(8,128)S(1)}, u32[]{:S(2)}, u32[]{:S(2)}) %collective-permute-start.14) | collective-permute-done | bytes 65568 | tf_op jit(solution)/shard_map/ppermute | solution.py:32
  55.3 2.2 %collective-permute-start.5 = (f32[64,256]{1,0:T(8,128)S(1)}, f32[64,256]{1,0:T(8,128)S(1)}, u32[]{:S(2)}, u32[]{:S(2)}) collective-permute-start(f32[64,256]{1,0:T(8,128)S(1)} %fusion.179), channel_id=1, source_target_pairs={{0,2},{1,3},{2,0},{3,1},{4,6},{5,7},{6,4},{7,5},{8,10},{9,11},{10,... | collective-permute-start | bytes 196616 | tf_op jit(solution)/shard_map/ppermute | solution.py:32
  57.6 1.6 %collective-permute-done.15 = f32[64,256]{1,0:T(8,128)S(1)} collective-permute-done((f32[64,256]{1,0:T(8,128)S(1)}, f32[64,256]{1,0:T(8,128)S(1)}, u32[]{:S(2)}, u32[]{:S(2)}) %collective-permute-start.15) | collective-permute-done | bytes 65568 | tf_op jit(solution)/shard_map/ppermute | solution.py:32
  61.9 2.4 %collective-permute-start.8 = (f32[64,256]{1,0:T(8,128)S(1)}, f32[64,256]{1,0:T(8,128)S(1)}, u32[]{:S(2)}, u32[]{:S(2)}) collective-permute-start(f32[64,256]{1,0:T(8,128)S(1)} %slice_add_fusion.13), channel_id=1, source_target_pairs={{0,1},{1,0},{2,3},{3,2},{4,5},{5,4},{6,7},{7,6},{8,9},{9,8},{10,11... | collective-permute-start | bytes 196616 | tf_op jit(solution)/shard_map/ppermute | solution.py:32
  65.1 1.7 %collective-permute-start.17 = (f32[64,256]{1,0:T(8,128)S(1)}, f32[64,256]{1,0:T(8,128)S(1)}, u32[]{:S(2)}, u32[]{:S(2)}) collective-permute-start(f32[64,256]{1,0:T(8,128)S(1)} %fusion.182), channel_id=1, source_target_pairs={{0,2},{1,3},{2,0},{3,1},{4,6},{5,7},{6,4},{7,5},{8,10},{9,11},{10,... | collective-permute-start | bytes 196616 | tf_op jit(solution)/shard_map/ppermute | solution.py:32
  66.9 2.9 %collective-permute-start.9 = (f32[64,256]{1,0:T(8,128)S(1)}, f32[64,256]{1,0:T(8,128)S(1)}, u32[]{:S(2)}, u32[]{:S(2)}) collective-permute-start(f32[64,256]{1,0:T(8,128)S(1)} %fusion.178), channel_id=1, source_target_pairs={{0,2},{1,3},{2,0},{3,1},{4,6},{5,7},{6,4},{7,5},{8,10},{9,11},{10,... | collective-permute-start | bytes 196616 | tf_op jit(solution)/shard_map/ppermute | solution.py:32
  71.9 2.0 %collective-permute-done.9 = f32[64,256]{1,0:T(8,128)S(1)} collective-permute-done((f32[64,256]{1,0:T(8,128)S(1)}, f32[64,256]{1,0:T(8,128)S(1)}, u32[]{:S(2)}, u32[]{:S(2)}) %collective-permute-start.9) | collective-permute-done | bytes 65568 | tf_op jit(solution)/shard_map/ppermute | solution.py:32
  76.3 3.0 %collective-permute-start.19 = (f32[64,256]{1,0:T(8,128)S(1)}, f32[64,256]{1,0:T(8,128)S(1)}, u32[]{:S(2)}, u32[]{:S(2)}) collective-permute-start(f32[64,256]{1,0:T(8,128)S(1)} %fusion.181), channel_id=1, source_target_pairs={{0,2},{1,3},{2,0},{3,1},{4,6},{5,7},{6,4},{7,5},{8,10},{9,11},{10,... | collective-permute-start | bytes 196616 | tf_op jit(solution)/shard_map/ppermute | solution.py:32
  79.5 2.1 %collective-permute-start.11 = (f32[64,256]{1,0:T(8,128)S(1)}, f32[64,256]{1,0:T(8,128)S(1)}, u32[]{:S(2)}, u32[]{:S(2)}) collective-permute-start(f32[64,256]{1,0:T(8,128)S(1)} %fusion.177), channel_id=1, source_target_pairs={{0,2},{1,3},{2,0},{3,1},{4,6},{5,7},{6,4},{7,5},{8,10},{9,11},{10,... | collective-permute-start | bytes 196616 | tf_op jit(solution)/shard_map/ppermute | solution.py:32
  83.0 1.7 %collective-permute-done.11 = f32[64,256]{1,0:T(8,128)S(1)} collective-permute-done((f32[64,256]{1,0:T(8,128)S(1)}, f32[64,256]{1,0:T(8,128)S(1)}, u32[]{:S(2)}, u32[]{:S(2)}) %collective-permute-start.11) | collective-permute-done | bytes 65568 | tf_op jit(solution)/shard_map/ppermute | solution.py:32
  85.4 1.1 %pad_maximum_fusion = f32[8,16,2048]{2,1,0:T(8,128)} fusion(f32[4,16,2048]{2,1,0:T(8,128)S(1)} %bitcast.76, f32[4,16,2048]{2,1,0:T(8,128)S(1)} %bitcast.77), kind=kLoop, calls=%fused_computation.8 | loop fusion | flops 262144 | bytes 2097152 | tf_op jit(solution)/shard_map/concatenate | solution.py:104
  86.4 3.7 %all-to-all-start.1 = ((f32[8,16,2048]{2,1,0:T(8,128)}), f32[8,16,2048]{2,1,0:T(8,128)S(1)}, u32[]{:S(2)}, u32[]{:S(2)}) async-start(f32[8,16,2048]{2,1,0:T(8,128)} %pad_maximum_fusion), calls=%async_computation.1 | async-start | bytes 2097152 | tf_op jit(solution)/shard_map/all_to_all | solution.py:103
  90.2 15.3 %all-to-all-done.1 = f32[8,16,2048]{2,1,0:T(8,128)S(1)} async-done(((f32[8,16,2048]{2,1,0:T(8,128)}), f32[8,16,2048]{2,1,0:T(8,128)S(1)}, u32[]{:S(2)}, u32[]{:S(2)}) %all-to-all-start.1) | async-done | bytes 1048608 | tf_op jit(solution)/shard_map/all_to_all | solution.py:103
  105.5 1.1 %select_bitcast_fusion = f32[1,8,16,2048]{3,2,1,0:T(8,128)} fusion(f32[8,16,2048]{2,1,0:T(8,128)S(1)} %all-to-all-done.1, pred[8,16]{1,0:T(8,128)(4,1)S(1)} %iota_compare_fusion.2), kind=kLoop, calls=%fused_computation.9 | loop fusion | flops 262144 | bytes 2097280 | tf_op jit(solution)/shard_map/broadcast_in_dim | solution.py:106
  (96 shorter events, 19.4 us)
Async XLA Ops:
  3.1 4.1 %copy-start = (bf16[1024,2048]{1,0:T(8,128)(2,1)}, bf16[1024,2048]{1,0:T(8,128)(2,1)S(1)}, u32[]{:S(2)}) copy-start(bf16[1024,2048]{1,0:T(8,128)(2,1)S(1)} %bitcast_select_fusion) | copy-start | bytes 12582916
  4.1 13.5 %collective-permute-start.6 = (f32[3,128,128]{2,1,0:T(8,128)S(1)}, f32[3,128,128]{2,1,0:T(8,128)S(1)}, u32[]{:S(2)}, u32[]{:S(2)}) collective-permute-start(f32[3,128,128]{2,1,0:T(8,128)S(1)} %pad_maximum_fusion.1), channel_id=1, source_target_pairs={{0,1},{1,0},{2,3},{3,2},{4,5},{5,4},{6,7},{7,6},{8,9},{9,8},{10,11... | collective-permute-start | bytes 589832 | tf_op jit(solution)/shard_map/ppermute | solution.py:32
  7.5 7.4 %collective-permute-start.2 = (f32[1,128,128]{2,1,0:T(8,128)S(1)}, f32[1,128,128]{2,1,0:T(8,128)S(1)}, u32[]{:S(2)}, u32[]{:S(2)}) collective-permute-start(f32[1,128,128]{2,1,0:T(8,128)S(1)} %convolution_bitcast_fusion.3), channel_id=1, source_target_pairs={{0,1},{1,0},{2,3},{3,2},{4,5},{5,4},{6,7},{7,6},{8,9},{9,8},{10,11... | collective-permute-start | bytes 196616 | tf_op jit(solution)/shard_map/ppermute | solution.py:32
  8.5 25.3 %all-to-all-start = ((f32[8,16,2048]{2,1,0:T(8,128)}), f32[8,16,2048]{2,1,0:T(8,128)S(1)}, u32[]{:S(2)}, u32[]{:S(2)}) async-start(f32[8,16,2048]{2,1,0:T(8,128)} %bitcast.1), calls=%async_computation | async-start | bytes 2097152 | tf_op jit(solution)/shard_map/all_to_all | solution.py:60
  14.9 11.5 %collective-permute-start.3 = (f32[1,128,128]{2,1,0:T(8,128)S(1)}, f32[1,128,128]{2,1,0:T(8,128)S(1)}, u32[]{:S(2)}, u32[]{:S(2)}) collective-permute-start(f32[1,128,128]{2,1,0:T(8,128)S(1)} %add.127), channel_id=1, source_target_pairs={{0,2},{1,3},{2,0},{3,1},{4,6},{5,7},{6,4},{7,5},{8,10},{9,11},{10,... | collective-permute-start | bytes 196616 | tf_op jit(solution)/shard_map/ppermute | solution.py:32
  17.6 12.6 %collective-permute-start.7 = (f32[3,128,128]{2,1,0:T(8,128)S(1)}, f32[3,128,128]{2,1,0:T(8,128)S(1)}, u32[]{:S(2)}, u32[]{:S(2)}) collective-permute-start(f32[3,128,128]{2,1,0:T(8,128)S(1)} %fusion.165), channel_id=1, source_target_pairs={{0,2},{1,3},{2,0},{3,1},{4,6},{5,7},{6,4},{7,5},{8,10},{9,11},{10,... | collective-permute-start | bytes 589832 | tf_op jit(solution)/shard_map/ppermute | solution.py:32
  33.9 2.2 %copy-start.1 = (bf16[1024,2048]{1,0:T(8,128)(2,1)S(1)}, bf16[1024,2048]{1,0:T(8,128)(2,1)}, u32[]{:S(2)}) copy-start(bf16[1024,2048]{1,0:T(8,128)(2,1)} %copy-done) | copy-start | bytes 12582916
  34.0 13.7 %copy-start.2 = (f32[1,128,128]{2,1,0:T(8,128)S(1)}, f32[1,128,128]{2,1,0:T(8,128)}, u32[]{:S(2)}) copy-start(f32[1,128,128]{2,1,0:T(8,128)} %get-tuple-element.9) | copy-start | bytes 196612
  34.0 13.7 %copy-start.3 = (f32[1,128,128]{2,1,0:T(8,128)S(1)}, f32[1,128,128]{2,1,0:T(8,128)}, u32[]{:S(2)}) copy-start(f32[1,128,128]{2,1,0:T(8,128)} %get-tuple-element.10) | copy-start | bytes 196612
  36.6 4.5 %collective-permute-start.12 = (f32[64,256]{1,0:T(8,128)S(1)}, f32[64,256]{1,0:T(8,128)S(1)}, u32[]{:S(2)}, u32[]{:S(2)}) collective-permute-start(f32[64,256]{1,0:T(8,128)S(1)} %slice_add_fusion.11), channel_id=1, source_target_pairs={{0,1},{1,0},{2,3},{3,2},{4,5},{5,4},{6,7},{7,6},{8,9},{9,8},{10,11... | collective-permute-start | bytes 196616 | tf_op jit(solution)/shard_map/ppermute | solution.py:32
  37.4 5.2 %collective-permute-start = (f32[64,256]{1,0:T(8,128)S(1)}, f32[64,256]{1,0:T(8,128)S(1)}, u32[]{:S(2)}, u32[]{:S(2)}) collective-permute-start(f32[64,256]{1,0:T(8,128)S(1)} %slice_add_fusion.15), channel_id=1, source_target_pairs={{0,1},{1,0},{2,3},{3,2},{4,5},{5,4},{6,7},{7,6},{8,9},{9,8},{10,11... | collective-permute-start | bytes 196616 | tf_op jit(solution)/shard_map/ppermute | solution.py:32
  41.1 6.6 %collective-permute-start.13 = (f32[64,256]{1,0:T(8,128)S(1)}, f32[64,256]{1,0:T(8,128)S(1)}, u32[]{:S(2)}, u32[]{:S(2)}) collective-permute-start(f32[64,256]{1,0:T(8,128)S(1)} %fusion.184), channel_id=1, source_target_pairs={{0,2},{1,3},{2,0},{3,1},{4,6},{5,7},{6,4},{7,5},{8,10},{9,11},{10,... | collective-permute-start | bytes 196616 | tf_op jit(solution)/shard_map/ppermute | solution.py:32
  42.6 6.4 %collective-permute-start.1 = (f32[64,256]{1,0:T(8,128)S(1)}, f32[64,256]{1,0:T(8,128)S(1)}, u32[]{:S(2)}, u32[]{:S(2)}) collective-permute-start(f32[64,256]{1,0:T(8,128)S(1)} %fusion.180), channel_id=1, source_target_pairs={{0,2},{1,3},{2,0},{3,1},{4,6},{5,7},{6,4},{7,5},{8,10},{9,11},{10,... | collective-permute-start | bytes 196616 | tf_op jit(solution)/shard_map/ppermute | solution.py:32
  48.9 4.9 %collective-permute-start.14 = (f32[64,256]{1,0:T(8,128)S(1)}, f32[64,256]{1,0:T(8,128)S(1)}, u32[]{:S(2)}, u32[]{:S(2)}) collective-permute-start(f32[64,256]{1,0:T(8,128)S(1)} %slice_add_fusion.10), channel_id=1, source_target_pairs={{0,1},{1,0},{2,3},{3,2},{4,5},{5,4},{6,7},{7,6},{8,9},{9,8},{10,11... | collective-permute-start | bytes 196616 | tf_op jit(solution)/shard_map/ppermute | solution.py:32
  50.3 5.0 %collective-permute-start.4 = (f32[64,256]{1,0:T(8,128)S(1)}, f32[64,256]{1,0:T(8,128)S(1)}, u32[]{:S(2)}, u32[]{:S(2)}) collective-permute-start(f32[64,256]{1,0:T(8,128)S(1)} %slice_add_fusion.14), channel_id=1, source_target_pairs={{0,1},{1,0},{2,3},{3,2},{4,5},{5,4},{6,7},{7,6},{8,9},{9,8},{10,11... | collective-permute-start | bytes 196616 | tf_op jit(solution)/shard_map/ppermute | solution.py:32
  53.9 5.2 %collective-permute-start.15 = (f32[64,256]{1,0:T(8,128)S(1)}, f32[64,256]{1,0:T(8,128)S(1)}, u32[]{:S(2)}, u32[]{:S(2)}) collective-permute-start(f32[64,256]{1,0:T(8,128)S(1)} %fusion.183), channel_id=1, source_target_pairs={{0,2},{1,3},{2,0},{3,1},{4,6},{5,7},{6,4},{7,5},{8,10},{9,11},{10,... | collective-permute-start | bytes 196616 | tf_op jit(solution)/shard_map/ppermute | solution.py:32
  55.3 5.3 %collective-permute-start.5 = (f32[64,256]{1,0:T(8,128)S(1)}, f32[64,256]{1,0:T(8,128)S(1)}, u32[]{:S(2)}, u32[]{:S(2)}) collective-permute-start(f32[64,256]{1,0:T(8,128)S(1)} %fusion.179), channel_id=1, source_target_pairs={{0,2},{1,3},{2,0},{3,1},{4,6},{5,7},{6,4},{7,5},{8,10},{9,11},{10,... | collective-permute-start | bytes 196616 | tf_op jit(solution)/shard_map/ppermute | solution.py:32
  60.4 4.7 %collective-permute-start.16 = (f32[64,256]{1,0:T(8,128)S(1)}, f32[64,256]{1,0:T(8,128)S(1)}, u32[]{:S(2)}, u32[]{:S(2)}) collective-permute-start(f32[64,256]{1,0:T(8,128)S(1)} %slice_add_fusion.9), channel_id=1, source_target_pairs={{0,1},{1,0},{2,3},{3,2},{4,5},{5,4},{6,7},{7,6},{8,9},{9,8},{10,11... | collective-permute-start | bytes 196616 | tf_op jit(solution)/shard_map/ppermute | solution.py:32
  61.9 4.9 %collective-permute-start.8 = (f32[64,256]{1,0:T(8,128)S(1)}, f32[64,256]{1,0:T(8,128)S(1)}, u32[]{:S(2)}, u32[]{:S(2)}) collective-permute-start(f32[64,256]{1,0:T(8,128)S(1)} %slice_add_fusion.13), channel_id=1, source_target_pairs={{0,1},{1,0},{2,3},{3,2},{4,5},{5,4},{6,7},{7,6},{8,9},{9,8},{10,11... | collective-permute-start | bytes 196616 | tf_op jit(solution)/shard_map/ppermute | solution.py:32
  65.1 5.5 %collective-permute-start.17 = (f32[64,256]{1,0:T(8,128)S(1)}, f32[64,256]{1,0:T(8,128)S(1)}, u32[]{:S(2)}, u32[]{:S(2)}) collective-permute-start(f32[64,256]{1,0:T(8,128)S(1)} %fusion.182), channel_id=1, source_target_pairs={{0,2},{1,3},{2,0},{3,1},{4,6},{5,7},{6,4},{7,5},{8,10},{9,11},{10,... | collective-permute-start | bytes 196616 | tf_op jit(solution)/shard_map/ppermute | solution.py:32
  66.9 7.0 %collective-permute-start.9 = (f32[64,256]{1,0:T(8,128)S(1)}, f32[64,256]{1,0:T(8,128)S(1)}, u32[]{:S(2)}, u32[]{:S(2)}) collective-permute-start(f32[64,256]{1,0:T(8,128)S(1)} %fusion.178), channel_id=1, source_target_pairs={{0,2},{1,3},{2,0},{3,1},{4,6},{5,7},{6,4},{7,5},{8,10},{9,11},{10,... | collective-permute-start | bytes 196616 | tf_op jit(solution)/shard_map/ppermute | solution.py:32
  71.8 4.5 %collective-permute-start.18 = (f32[64,256]{1,0:T(8,128)S(1)}, f32[64,256]{1,0:T(8,128)S(1)}, u32[]{:S(2)}, u32[]{:S(2)}) collective-permute-start(f32[64,256]{1,0:T(8,128)S(1)} %slice_add_fusion.8), channel_id=1, source_target_pairs={{0,1},{1,0},{2,3},{3,2},{4,5},{5,4},{6,7},{7,6},{8,9},{9,8},{10,11... | collective-permute-start | bytes 196616 | tf_op jit(solution)/shard_map/ppermute | solution.py:32
  75.1 4.3 %collective-permute-start.10 = (f32[64,256]{1,0:T(8,128)S(1)}, f32[64,256]{1,0:T(8,128)S(1)}, u32[]{:S(2)}, u32[]{:S(2)}) collective-permute-start(f32[64,256]{1,0:T(8,128)S(1)} %slice_add_fusion.12), channel_id=1, source_target_pairs={{0,1},{1,0},{2,3},{3,2},{4,5},{5,4},{6,7},{7,6},{8,9},{9,8},{10,11... | collective-permute-start | bytes 196616 | tf_op jit(solution)/shard_map/ppermute | solution.py:32
  76.3 6.0 %collective-permute-start.19 = (f32[64,256]{1,0:T(8,128)S(1)}, f32[64,256]{1,0:T(8,128)S(1)}, u32[]{:S(2)}, u32[]{:S(2)}) collective-permute-start(f32[64,256]{1,0:T(8,128)S(1)} %fusion.181), channel_id=1, source_target_pairs={{0,2},{1,3},{2,0},{3,1},{4,6},{5,7},{6,4},{7,5},{8,10},{9,11},{10,... | collective-permute-start | bytes 196616 | tf_op jit(solution)/shard_map/ppermute | solution.py:32
  79.5 5.2 %collective-permute-start.11 = (f32[64,256]{1,0:T(8,128)S(1)}, f32[64,256]{1,0:T(8,128)S(1)}, u32[]{:S(2)}, u32[]{:S(2)}) collective-permute-start(f32[64,256]{1,0:T(8,128)S(1)} %fusion.177), channel_id=1, source_target_pairs={{0,2},{1,3},{2,0},{3,1},{4,6},{5,7},{6,4},{7,5},{8,10},{9,11},{10,... | collective-permute-start | bytes 196616 | tf_op jit(solution)/shard_map/ppermute | solution.py:32
  85.0 5.2 %copy-start.4 = (s32[1,8]{1,0:T(1,128)S(1)}, s32[1,8]{1,0:T(1,128)}, u32[]{:S(2)}) copy-start(s32[1,8]{1,0:T(1,128)} %param.11) | copy-start | bytes 100
  86.4 19.1 %all-to-all-start.1 = ((f32[8,16,2048]{2,1,0:T(8,128)}), f32[8,16,2048]{2,1,0:T(8,128)S(1)}, u32[]{:S(2)}, u32[]{:S(2)}) async-start(f32[8,16,2048]{2,1,0:T(8,128)} %pad_maximum_fusion), calls=%async_computation.1 | async-start | bytes 2097152 | tf_op jit(solution)/shard_map/all_to_all | solution.py:103

commit v4 on v3

--- a/solution.py
+++ b/solution.py
@@ -69,6 +69,7 @@
     def product(pair):
         return dot(span(2 * pair + 1, 2 * pair + 2), span(2 * pair, 2 * pair + 1), ROWS)
 
+    last_pair = lax.optimization_barrier(span(count - 2, count))
     gram_first = total(product(turns[0])[None], "section")
     rest = jnp.stack([product(pair) for pair in turns[1:]])
     gram_rest = total(rest, "section")
@@ -89,21 +90,28 @@
     rest = merge(gram_rest, *turned[2:])
     merged += [rest[index] for index in range(pairs - 1)]
 
-    half = held.shape[0] // 2
-    panels = [held[number * half:(number + 1) * half].reshape(half * slots, rows) for number in range(2)]
+    peers, half = held.shape[0], held.shape[0] // 2
+    me = lax.axis_index("group")
+    top = me // half
+    panels = []
+    for side in (top, 1 - top):
+        panels.append(lax.dynamic_slice_in_dim(held, side * half, half, 0).reshape(half * slots, rows))
     for index, pair in enumerate(turns):
         vectors_of = span(2 * pair, 2 * pair + 2)
         for number, panel in enumerate(panels):
-            inner = folded(dot(split(panel), vectors_of, ROWS))
+            inner = folded(dot(split(panel), vectors_of if index else last_pair, ROWS))
             inner = total(inner, "section")
             weights = dot(inner, merged[index], INNER, HIGH)
             panels[number] = panel - folded(dot(split(weights), vectors_of, INNER))
-    moved = [panel.reshape(half, slots, rows) for panel in panels]
-
-    returned = lax.all_to_all(
-        jnp.concatenate(moved, axis=0), "group", split_axis=0, concat_axis=0, tiled=True)
+    result = jnp.zeros_like(held)
+    for step in reversed(range(peers)):
+        home = me ^ step
+        block = lax.dynamic_slice_in_dim(panels[step // half], (home % half) * slots, slots, 0)
+        if step:
+            block = lax.ppermute(block, "group", [(i, i ^ step) for i in range(peers)])
+        result = lax.dynamic_update_slice_in_dim(result, block[None], home, 0)
     keep = jnp.arange(slots)[None, :] < live[0][:, None]
-    return jnp.where(keep[:, :, None], returned, jnp.float32(0.0))[None]
+    return jnp.where(keep[:, :, None], result, jnp.float32(0.0))[None]
 
 
 def solution(mesh):

time: 107 us -> 102 us (0.953)
  waiting for transfers between devices: 39.9 us -> 35.3 us
    all_to_all x1 -> x0, waiting for transfers between devices: 15.3 us -> none  [shards(): lax.all_to_all(jnp.concatenate(moved, axis=0), 'group', split_axis=0, con...]
    ppermute x0 -> x7, waiting for transfers between devices: none -> 11 us  [shards(): block = lax.ppermute(block, 'group', [(i, i ^ step) for i in range(peers)])]
    ppermute x0 -> x7, starting transfers between devices: none -> 7.48 us  [shards(): block = lax.ppermute(block, 'group', [(i, i ^ step) for i in range(peers)])]
    ppermute x20, starting transfers between devices: 32 us -> 27.7 us  [exchange(): return lax.ppermute(value, axis, [(i, i ^ step) for i in range(count)])]
    all_to_all x1 -> x0, starting transfers between devices: 3.67 us -> none  [shards(): lax.all_to_all(jnp.concatenate(moved, axis=0), 'group', split_axis=0, con...]
    unnamed x10, local copies, waits for them, and re-layouts: 1.95 us -> 0.02 us
    all_to_all x1, starting transfers between devices: 3.72 us -> 5.2 us  [shards(): lax.all_to_all(columns[0], 'group', split_axis=0, concat_axis=0, tiled=True)]
    slice x1, local copies, waits for them, and re-layouts: 0.07 us -> 1.29 us  [span(): return basis[low * width:high * width]]
  transfers between devices with their start and end apart: 22 -> 28, of which waited for: 16 -> 18; matrix products, arithmetic and copies ran while one was open for 14% -> 20% of each run, Pallas kernels for 2% -> 2%
where the time goes in v4:
time: 102 us
  starting transfers between devices  40.4 us (40%)
  waiting for transfers between devices  35.3 us (35%)
  matrix products  14.2 us (14%)
  other arithmetic  6.11 us (6%)
  between operations  2.25 us (2%)
  Pallas kernels  1.99 us (2%)
  local copies, waits for them, and re-layouts  1.71 us (2%)
    ppermute x20, starting transfers between devices, exchange(): return lax.ppermute(value, axis, [(i, i ^ step) for i in range(count)])  27.7 us
    ppermute x20, waiting for transfers between devices, exchange(): return lax.ppermute(value, axis, [(i, i ^ step) for i in range(count)])  24.3 us
    ppermute x7, waiting for transfers between devices, shards(): block = lax.ppermute(block, 'group', [(i, i ^ step) for i in range(peers)])  11 us
    dot_general x28, matrix products, dot(): lax.dot_general(left, right, (dims, ((), ())), precision=precision, prefe...  9.58 us
    ppermute x7, starting transfers between devices, shards(): block = lax.ppermute(block, 'group', [(i, i ^ step) for i in range(peers)])  7.48 us
    all_to_all x1, starting transfers between devices, shards(): lax.all_to_all(columns[0], 'group', split_axis=0, concat_axis=0, tiled=True)  5.2 us
    select_n x1, other arithmetic, shards(): jnp.where(inside[None, :], vectors[0].reshape(count * width, rows), jnp.b...  2.47 us
    dot_general x2, matrix products, merge(): lax.dot_general(higher, gram, batch, precision=HIGH)  2.31 us
  transfers between devices with their start and end apart: 28, of which 18 were waited for; matrix products, arithmetic and copies ran while one was open for 20% of the time, Pallas kernels for 2%

profile of v4, /device:TPU:0, one launch (start us, length us, event | category | flops | bytes accessed | tf_op | source)
XLA Modules:
  0.0 102.0 jit_solution(2620206330737646422)
XLA Ops:
  0.0 5.2 %all-to-all-start = ((f32[8,16,2048]{2,1,0:T(8,128)}), f32[8,16,2048]{2,1,0:T(8,128)S(1)}, u32[]{:S(2)}, u32[]{:S(2)}) async-start(f32[8,16,2048]{2,1,0:T(8,128)} %bitcast.92), calls=%async_computation | async-start | bytes 2097152 | tf_op jit(solution)/shard_map/all_to_all | solution.py:60
  5.9 2.5 %bitcast_select_fusion = bf16[1024,2048]{1,0:T(8,128)(2,1)S(1)} fusion(bf16[1,8,128,2048]{3,2,1,0:T(8,128)(2,1)} %param.7, pred[2048]{0:T(1024)(128)(4,1)S(1)} %add_compare_fusion), kind=kLoop, calls=%fused_computation | loop fusion | flops 2097152 | bytes 8390656 | tf_op jit(solution)/shard_map/jit(_where)/select_n | solution.py:63
  8.7 1.6 %collective-permute-start.2 = (f32[1,128,128]{2,1,0:T(8,128)S(1)}, f32[1,128,128]{2,1,0:T(8,128)S(1)}, u32[]{:S(2)}, u32[]{:S(2)}) collective-permute-start(f32[1,128,128]{2,1,0:T(8,128)S(1)} %convolution_bitcast_fusion.3), channel_id=1, source_target_pairs={{0,1},{1,0},{2,3},{3,2},{4,5},{5,4},{6,7},{7,6},{8,9},{9,8},{10,11... | collective-permute-start | bytes 196616 | tf_op jit(solution)/shard_map/ppermute | solution.py:32
  12.5 1.3 %slice.189 = bf16[256,2048]{1,0:T(8,128)(2,1)S(1)} slice(bf16[1024,2048]{1,0:T(8,128)(2,1)} %copy-done), slice={[768:1024], [0:2048]} | slice | bytes 2097152 | tf_op jit(solution)/shard_map/slice | solution.py:67
  14.5 2.0 %turn.1 = (f32[1,128,128]{2,1,0:T(8,128)}, f32[1,128,128]{2,1,0:T(8,128)}, f32[3,128,128]{2,1,0:T(8,128)}, f32[3,128,128]{2,1,0:T(8,128)}) custom-call(s32[1]{0:T(128)S(6)} %copy.22.blocks_ref, f32[8,128,128]{2,1,0:T(8,128)} %bitcast.93), custom_call_target="tpu_custom_call" | custom-call | tf_op jit(solution)/shard_map/turn/pallas_call | solution.py:77
  16.5 2.7 %collective-permute-start.3 = (f32[1,128,128]{2,1,0:T(8,128)S(1)}, f32[1,128,128]{2,1,0:T(8,128)S(1)}, u32[]{:S(2)}, u32[]{:S(2)}) collective-permute-start(f32[1,128,128]{2,1,0:T(8,128)S(1)} %add.208), channel_id=1, source_target_pairs={{0,2},{1,3},{2,0},{3,1},{4,6},{5,7},{6,4},{7,5},{8,10},{9,11},{10,... | collective-permute-start | bytes 196616 | tf_op jit(solution)/shard_map/ppermute | solution.py:32
  19.2 1.8 %collective-permute-start.7 = (f32[3,128,128]{2,1,0:T(8,128)S(1)}, f32[3,128,128]{2,1,0:T(8,128)S(1)}, u32[]{:S(2)}, u32[]{:S(2)}) collective-permute-start(f32[3,128,128]{2,1,0:T(8,128)S(1)} %fusion.161), channel_id=1, source_target_pairs={{0,2},{1,3},{2,0},{3,1},{4,6},{5,7},{6,4},{7,5},{8,10},{9,11},{10,... | collective-permute-start | bytes 589832 | tf_op jit(solution)/shard_map/ppermute | solution.py:32
  21.0 6.7 %collective-permute-done.3 = f32[1,128,128]{2,1,0:T(8,128)S(1)} collective-permute-done((f32[1,128,128]{2,1,0:T(8,128)S(1)}, f32[1,128,128]{2,1,0:T(8,128)S(1)}, u32[]{:S(2)}, u32[]{:S(2)}) %collective-permute-start.3) | collective-permute-done | bytes 65568 | tf_op jit(solution)/shard_map/ppermute | solution.py:32
  29.8 1.8 %collective-permute-done.7 = f32[3,128,128]{2,1,0:T(8,128)S(1)} collective-permute-done((f32[3,128,128]{2,1,0:T(8,128)S(1)}, f32[3,128,128]{2,1,0:T(8,128)S(1)}, u32[]{:S(2)}, u32[]{:S(2)}) %collective-permute-start.7) | collective-permute-done | bytes 196640 | tf_op jit(solution)/shard_map/ppermute | solution.py:32
  31.6 1.3 %fusion.82 = f32[3,128,128]{2,1,0:T(8,128)S(1)} fusion(f32[3,128,128]{2,1,0:T(8,128)} %get-tuple-element.12, f32[3,128,128]{2,1,0:T(8,128)S(1)} %fusion.161, f32[3,128,128]{2,1,0:T(8,128)S(1)} %collective-permute-done.7), kind=kOutput, calls=%fused_computation.122 | convolution fusion | flops 75546624 | bytes 786432 | tf_op jit(solution)/shard_map/dot_general | solution.py:84
  32.8 1.3 %convolution_negate_fusion = f32[3,128,128]{2,1,0:T(8,128)S(1)} fusion(f32[3,128,128]{2,1,0:T(8,128)S(1)} %fusion.82, f32[3,128,128]{2,1,0:T(8,128)} %get-tuple-element.11), kind=kOutput, calls=%fused_computation.1 | convolution fusion | flops 75546624 | bytes 589824 | tf_op jit(solution)/shard_map/dot_general | solution.py:83
  36.6 2.1 %collective-permute-start.16 = (f32[64,256]{1,0:T(8,128)S(1)}, f32[64,256]{1,0:T(8,128)S(1)}, u32[]{:S(2)}, u32[]{:S(2)}) collective-permute-start(f32[64,256]{1,0:T(8,128)S(1)} %slice_add_fusion.11), channel_id=1, source_target_pairs={{0,1},{1,0},{2,3},{3,2},{4,5},{5,4},{6,7},{7,6},{8,9},{9,8},{10,11... | collective-permute-start | bytes 196616 | tf_op jit(solution)/shard_map/ppermute | solution.py:32
  38.7 1.9 %collective-permute-done = f32[64,256]{1,0:T(8,128)S(1)} collective-permute-done((f32[64,256]{1,0:T(8,128)S(1)}, f32[64,256]{1,0:T(8,128)S(1)}, u32[]{:S(2)}, u32[]{:S(2)}) %collective-permute-start) | collective-permute-done | bytes 65568 | tf_op jit(solution)/shard_map/ppermute | solution.py:32
  40.6 1.2 %collective-permute-start.1 = (f32[64,256]{1,0:T(8,128)S(1)}, f32[64,256]{1,0:T(8,128)S(1)}, u32[]{:S(2)}, u32[]{:S(2)}) collective-permute-start(f32[64,256]{1,0:T(8,128)S(1)} %fusion.183), channel_id=1, source_target_pairs={{0,2},{1,3},{2,0},{3,1},{4,6},{5,7},{6,4},{7,5},{8,10},{9,11},{10,... | collective-permute-start | bytes 196616 | tf_op jit(solution)/shard_map/ppermute | solution.py:32
  41.8 2.7 %collective-permute-start.17 = (f32[64,256]{1,0:T(8,128)S(1)}, f32[64,256]{1,0:T(8,128)S(1)}, u32[]{:S(2)}, u32[]{:S(2)}) collective-permute-start(f32[64,256]{1,0:T(8,128)S(1)} %fusion.179), channel_id=1, source_target_pairs={{0,2},{1,3},{2,0},{3,1},{4,6},{5,7},{6,4},{7,5},{8,10},{9,11},{10,... | collective-permute-start | bytes 196616 | tf_op jit(solution)/shard_map/ppermute | solution.py:32
  44.5 2.4 %collective-permute-done.1 = f32[64,256]{1,0:T(8,128)S(1)} collective-permute-done((f32[64,256]{1,0:T(8,128)S(1)}, f32[64,256]{1,0:T(8,128)S(1)}, u32[]{:S(2)}, u32[]{:S(2)}) %collective-permute-start.1) | collective-permute-done | bytes 65568 | tf_op jit(solution)/shard_map/ppermute | solution.py:32
  49.5 2.1 %collective-permute-start.18 = (f32[64,256]{1,0:T(8,128)S(1)}, f32[64,256]{1,0:T(8,128)S(1)}, u32[]{:S(2)}, u32[]{:S(2)}) collective-permute-start(f32[64,256]{1,0:T(8,128)S(1)} %slice_add_fusion.10), channel_id=1, source_target_pairs={{0,1},{1,0},{2,3},{3,2},{4,5},{5,4},{6,7},{7,6},{8,9},{9,8},{10,11... | collective-permute-start | bytes 196616 | tf_op jit(solution)/shard_map/ppermute | solution.py:32
  51.6 1.5 %collective-permute-done.4 = f32[64,256]{1,0:T(8,128)S(1)} collective-permute-done((f32[64,256]{1,0:T(8,128)S(1)}, f32[64,256]{1,0:T(8,128)S(1)}, u32[]{:S(2)}, u32[]{:S(2)}) %collective-permute-start.4) | collective-permute-done | bytes 65568 | tf_op jit(solution)/shard_map/ppermute | solution.py:32
  54.6 2.0 %collective-permute-start.19 = (f32[64,256]{1,0:T(8,128)S(1)}, f32[64,256]{1,0:T(8,128)S(1)}, u32[]{:S(2)}, u32[]{:S(2)}) collective-permute-start(f32[64,256]{1,0:T(8,128)S(1)} %fusion.178), channel_id=1, source_target_pairs={{0,2},{1,3},{2,0},{3,1},{4,6},{5,7},{6,4},{7,5},{8,10},{9,11},{10,... | collective-permute-start | bytes 196616 | tf_op jit(solution)/shard_map/ppermute | solution.py:32
  56.6 1.8 %collective-permute-done.5 = f32[64,256]{1,0:T(8,128)S(1)} collective-permute-done((f32[64,256]{1,0:T(8,128)S(1)}, f32[64,256]{1,0:T(8,128)S(1)}, u32[]{:S(2)}, u32[]{:S(2)}) %collective-permute-start.5) | collective-permute-done | bytes 65568 | tf_op jit(solution)/shard_map/ppermute | solution.py:32
  61.1 2.2 %collective-permute-start.20 = (f32[64,256]{1,0:T(8,128)S(1)}, f32[64,256]{1,0:T(8,128)S(1)}, u32[]{:S(2)}, u32[]{:S(2)}) collective-permute-start(f32[64,256]{1,0:T(8,128)S(1)} %slice_add_fusion.9), channel_id=1, source_target_pairs={{0,1},{1,0},{2,3},{3,2},{4,5},{5,4},{6,7},{7,6},{8,9},{9,8},{10,11... | collective-permute-start | bytes 196616 | tf_op jit(solution)/shard_map/ppermute | solution.py:32
  63.3 1.3 %collective-permute-done.8 = f32[64,256]{1,0:T(8,128)S(1)} collective-permute-done((f32[64,256]{1,0:T(8,128)S(1)}, f32[64,256]{1,0:T(8,128)S(1)}, u32[]{:S(2)}, u32[]{:S(2)}) %collective-permute-start.8) | collective-permute-done | bytes 65568 | tf_op jit(solution)/shard_map/ppermute | solution.py:32
  65.6 3.1 %collective-permute-start.21 = (f32[64,256]{1,0:T(8,128)S(1)}, f32[64,256]{1,0:T(8,128)S(1)}, u32[]{:S(2)}, u32[]{:S(2)}) collective-permute-start(f32[64,256]{1,0:T(8,128)S(1)} %fusion.177), channel_id=1, source_target_pairs={{0,2},{1,3},{2,0},{3,1},{4,6},{5,7},{6,4},{7,5},{8,10},{9,11},{10,... | collective-permute-start | bytes 196616 | tf_op jit(solution)/shard_map/ppermute | solution.py:32
  71.2 2.6 %collective-permute-done.21 = f32[64,256]{1,0:T(8,128)S(1)} collective-permute-done((f32[64,256]{1,0:T(8,128)S(1)}, f32[64,256]{1,0:T(8,128)S(1)}, u32[]{:S(2)}, u32[]{:S(2)}) %collective-permute-start.21) | collective-permute-done | bytes 65568 | tf_op jit(solution)/shard_map/ppermute | solution.py:32
  75.4 2.9 %collective-permute-start.11 = (f32[64,256]{1,0:T(8,128)S(1)}, f32[64,256]{1,0:T(8,128)S(1)}, u32[]{:S(2)}, u32[]{:S(2)}) collective-permute-start(f32[64,256]{1,0:T(8,128)S(1)} %fusion.180), channel_id=1, source_target_pairs={{0,2},{1,3},{2,0},{3,1},{4,6},{5,7},{6,4},{7,5},{8,10},{9,11},{10,... | collective-permute-start | bytes 196616 | tf_op jit(solution)/shard_map/ppermute | solution.py:32
  79.3 1.3 %collective-permute-start.23 = (f32[64,256]{1,0:T(8,128)S(1)}, f32[64,256]{1,0:T(8,128)S(1)}, u32[]{:S(2)}, u32[]{:S(2)}) collective-permute-start(f32[64,256]{1,0:T(8,128)S(1)} %fusion.176), channel_id=1, source_target_pairs={{0,2},{1,3},{2,0},{3,1},{4,6},{5,7},{6,4},{7,5},{8,10},{9,11},{10,... | collective-permute-start | bytes 196616 | tf_op jit(solution)/shard_map/ppermute | solution.py:32
  81.4 2.3 %collective-permute-start.15 = (f32[16,2048]{1,0:T(8,128)S(1)}, f32[16,2048]{1,0:T(8,128)S(1)}, u32[]{:S(2)}, u32[]{:S(2)}) collective-permute-start(f32[16,2048]{1,0:T(8,128)S(1)} %get-tuple-element.32), channel_id=1, source_target_pairs={{0,16},{4,20},{8,24},{12,28},{16,0},{20,4},{24,8},{28,12},{1,17},{... | collective-permute-start | bytes 393224 | tf_op jit(solution)/shard_map/ppermute | solution.py:111
  83.7 1.5 %collective-permute-start.13 = (f32[16,2048]{1,0:T(8,128)S(1)}, f32[16,2048]{1,0:T(8,128)S(1)}, u32[]{:S(2)}, u32[]{:S(2)}) collective-permute-start(f32[16,2048]{1,0:T(8,128)S(1)} %get-tuple-element.34), channel_id=1, source_target_pairs={{0,24},{4,28},{8,16},{12,20},{16,8},{20,12},{24,0},{28,4},{1,25},{... | collective-permute-start | bytes 393224 | tf_op jit(solution)/shard_map/ppermute | solution.py:111
  85.1 1.2 %collective-permute-start.12 = (f32[16,2048]{1,0:T(8,128)S(1)}, f32[16,2048]{1,0:T(8,128)S(1)}, u32[]{:S(2)}, u32[]{:S(2)}) collective-permute-start(f32[16,2048]{1,0:T(8,128)S(1)} %get-tuple-element.35), channel_id=1, source_target_pairs={{0,28},{4,24},{8,20},{12,16},{16,12},{20,8},{24,4},{28,0},{1,29},{... | collective-permute-start | bytes 393224 | tf_op jit(solution)/shard_map/ppermute | solution.py:111
  87.5 5.2 %collective-permute-done.12 = f32[16,2048]{1,0:T(8,128)S(1)} collective-permute-done((f32[16,2048]{1,0:T(8,128)S(1)}, f32[16,2048]{1,0:T(8,128)S(1)}, u32[]{:S(2)}, u32[]{:S(2)}) %collective-permute-start.12) | collective-permute-done | bytes 131104 | tf_op jit(solution)/shard_map/ppermute | solution.py:111
  92.7 2.0 %collective-permute-start.25 = (f32[16,2048]{1,0:T(8,128)S(1)}, f32[16,2048]{1,0:T(8,128)S(1)}, u32[]{:S(2)}, u32[]{:S(2)}) collective-permute-start(f32[16,2048]{1,0:T(8,128)S(1)} %get-tuple-element.28), channel_id=1, source_target_pairs={{0,8},{4,12},{8,0},{12,4},{16,24},{20,28},{24,16},{28,20},{1,9},{5... | collective-permute-start | bytes 393224 | tf_op jit(solution)/shard_map/ppermute | solution.py:111
  95.1 5.6 %collective-permute-done.24 = f32[16,2048]{1,0:T(8,128)S(1)} collective-permute-done((f32[16,2048]{1,0:T(8,128)S(1)}, f32[16,2048]{1,0:T(8,128)S(1)}, u32[]{:S(2)}, u32[]{:S(2)}) %collective-permute-start.24) | collective-permute-done | bytes 131104 | tf_op jit(solution)/shard_map/ppermute | solution.py:111
  (119 shorter events, 22.9 us)
Async XLA Ops:
  0.0 35.2 %all-to-all-start = ((f32[8,16,2048]{2,1,0:T(8,128)}), f32[8,16,2048]{2,1,0:T(8,128)S(1)}, u32[]{:S(2)}, u32[]{:S(2)}) async-start(f32[8,16,2048]{2,1,0:T(8,128)} %bitcast.92), calls=%async_computation | async-start | bytes 2097152 | tf_op jit(solution)/shard_map/all_to_all | solution.py:60
  8.3 3.9 %copy-start.4 = (s32[1,8]{1,0:T(1,128)S(1)}, s32[1,8]{1,0:T(1,128)}, u32[]{:S(2)}) copy-start(s32[1,8]{1,0:T(1,128)} %param.11) | copy-start | bytes 100
  8.7 7.9 %collective-permute-start.2 = (f32[1,128,128]{2,1,0:T(8,128)S(1)}, f32[1,128,128]{2,1,0:T(8,128)S(1)}, u32[]{:S(2)}, u32[]{:S(2)}) collective-permute-start(f32[1,128,128]{2,1,0:T(8,128)S(1)} %convolution_bitcast_fusion.3), channel_id=1, source_target_pairs={{0,1},{1,0},{2,3},{3,2},{4,5},{5,4},{6,7},{7,6},{8,9},{9,8},{10,11... | collective-permute-start | bytes 196616 | tf_op jit(solution)/shard_map/ppermute | solution.py:32
  11.3 7.9 %collective-permute-start.6 = (f32[3,128,128]{2,1,0:T(8,128)S(1)}, f32[3,128,128]{2,1,0:T(8,128)S(1)}, u32[]{:S(2)}, u32[]{:S(2)}) collective-permute-start(f32[3,128,128]{2,1,0:T(8,128)S(1)} %pad_maximum_fusion), channel_id=1, source_target_pairs={{0,1},{1,0},{2,3},{3,2},{4,5},{5,4},{6,7},{7,6},{8,9},{9,8},{10,11... | collective-permute-start | bytes 589832 | tf_op jit(solution)/shard_map/ppermute | solution.py:32
  16.5 11.1 %collective-permute-start.3 = (f32[1,128,128]{2,1,0:T(8,128)S(1)}, f32[1,128,128]{2,1,0:T(8,128)S(1)}, u32[]{:S(2)}, u32[]{:S(2)}) collective-permute-start(f32[1,128,128]{2,1,0:T(8,128)S(1)} %add.208), channel_id=1, source_target_pairs={{0,2},{1,3},{2,0},{3,1},{4,6},{5,7},{6,4},{7,5},{8,10},{9,11},{10,... | collective-permute-start | bytes 196616 | tf_op jit(solution)/shard_map/ppermute | solution.py:32
  19.2 12.3 %collective-permute-start.7 = (f32[3,128,128]{2,1,0:T(8,128)S(1)}, f32[3,128,128]{2,1,0:T(8,128)S(1)}, u32[]{:S(2)}, u32[]{:S(2)}) collective-permute-start(f32[3,128,128]{2,1,0:T(8,128)S(1)} %fusion.161), channel_id=1, source_target_pairs={{0,2},{1,3},{2,0},{3,1},{4,6},{5,7},{6,4},{7,5},{8,10},{9,11},{10,... | collective-permute-start | bytes 589832 | tf_op jit(solution)/shard_map/ppermute | solution.py:32
  35.2 11.7 %copy-start.2 = (f32[1,128,128]{2,1,0:T(8,128)S(1)}, f32[1,128,128]{2,1,0:T(8,128)}, u32[]{:S(2)}) copy-start(f32[1,128,128]{2,1,0:T(8,128)} %get-tuple-element.9) | copy-start | bytes 196612
  35.2 11.7 %copy-start.3 = (f32[1,128,128]{2,1,0:T(8,128)S(1)}, f32[1,128,128]{2,1,0:T(8,128)}, u32[]{:S(2)}) copy-start(f32[1,128,128]{2,1,0:T(8,128)} %get-tuple-element.10) | copy-start | bytes 196612
  35.2 11.9 %copy-start.1 = (bf16[1024,2048]{1,0:T(8,128)(2,1)S(1)}, bf16[1024,2048]{1,0:T(8,128)(2,1)}, u32[]{:S(2)}) copy-start(bf16[1024,2048]{1,0:T(8,128)(2,1)} %copy-done) | copy-start | bytes 12582916
  36.0 4.5 %collective-permute-start = (f32[64,256]{1,0:T(8,128)S(1)}, f32[64,256]{1,0:T(8,128)S(1)}, u32[]{:S(2)}, u32[]{:S(2)}) collective-permute-start(f32[64,256]{1,0:T(8,128)S(1)} %slice_add_fusion.15), channel_id=1, source_target_pairs={{0,1},{1,0},{2,3},{3,2},{4,5},{5,4},{6,7},{7,6},{8,9},{9,8},{10,11... | collective-permute-start | bytes 196616 | tf_op jit(solution)/shard_map/ppermute | solution.py:32
  36.6 5.2 %collective-permute-start.16 = (f32[64,256]{1,0:T(8,128)S(1)}, f32[64,256]{1,0:T(8,128)S(1)}, u32[]{:S(2)}, u32[]{:S(2)}) collective-permute-start(f32[64,256]{1,0:T(8,128)S(1)} %slice_add_fusion.11), channel_id=1, source_target_pairs={{0,1},{1,0},{2,3},{3,2},{4,5},{5,4},{6,7},{7,6},{8,9},{9,8},{10,11... | collective-permute-start | bytes 196616 | tf_op jit(solution)/shard_map/ppermute | solution.py:32
  40.6 6.3 %collective-permute-start.1 = (f32[64,256]{1,0:T(8,128)S(1)}, f32[64,256]{1,0:T(8,128)S(1)}, u32[]{:S(2)}, u32[]{:S(2)}) collective-permute-start(f32[64,256]{1,0:T(8,128)S(1)} %fusion.183), channel_id=1, source_target_pairs={{0,2},{1,3},{2,0},{3,1},{4,6},{5,7},{6,4},{7,5},{8,10},{9,11},{10,... | collective-permute-start | bytes 196616 | tf_op jit(solution)/shard_map/ppermute | solution.py:32
  41.8 6.4 %collective-permute-start.17 = (f32[64,256]{1,0:T(8,128)S(1)}, f32[64,256]{1,0:T(8,128)S(1)}, u32[]{:S(2)}, u32[]{:S(2)}) collective-permute-start(f32[64,256]{1,0:T(8,128)S(1)} %fusion.179), channel_id=1, source_target_pairs={{0,2},{1,3},{2,0},{3,1},{4,6},{5,7},{6,4},{7,5},{8,10},{9,11},{10,... | collective-permute-start | bytes 196616 | tf_op jit(solution)/shard_map/ppermute | solution.py:32
  48.2 4.9 %collective-permute-start.4 = (f32[64,256]{1,0:T(8,128)S(1)}, f32[64,256]{1,0:T(8,128)S(1)}, u32[]{:S(2)}, u32[]{:S(2)}) collective-permute-start(f32[64,256]{1,0:T(8,128)S(1)} %slice_add_fusion.14), channel_id=1, source_target_pairs={{0,1},{1,0},{2,3},{3,2},{4,5},{5,4},{6,7},{7,6},{8,9},{9,8},{10,11... | collective-permute-start | bytes 196616 | tf_op jit(solution)/shard_map/ppermute | solution.py:32
  49.5 5.0 %collective-permute-start.18 = (f32[64,256]{1,0:T(8,128)S(1)}, f32[64,256]{1,0:T(8,128)S(1)}, u32[]{:S(2)}, u32[]{:S(2)}) collective-permute-start(f32[64,256]{1,0:T(8,128)S(1)} %slice_add_fusion.10), channel_id=1, source_target_pairs={{0,1},{1,0},{2,3},{3,2},{4,5},{5,4},{6,7},{7,6},{8,9},{9,8},{10,11... | collective-permute-start | bytes 196616 | tf_op jit(solution)/shard_map/ppermute | solution.py:32
  53.1 5.2 %collective-permute-start.5 = (f32[64,256]{1,0:T(8,128)S(1)}, f32[64,256]{1,0:T(8,128)S(1)}, u32[]{:S(2)}, u32[]{:S(2)}) collective-permute-start(f32[64,256]{1,0:T(8,128)S(1)} %fusion.182), channel_id=1, source_target_pairs={{0,2},{1,3},{2,0},{3,1},{4,6},{5,7},{6,4},{7,5},{8,10},{9,11},{10,... | collective-permute-start | bytes 196616 | tf_op jit(solution)/shard_map/ppermute | solution.py:32
  54.6 5.3 %collective-permute-start.19 = (f32[64,256]{1,0:T(8,128)S(1)}, f32[64,256]{1,0:T(8,128)S(1)}, u32[]{:S(2)}, u32[]{:S(2)}) collective-permute-start(f32[64,256]{1,0:T(8,128)S(1)} %fusion.178), channel_id=1, source_target_pairs={{0,2},{1,3},{2,0},{3,1},{4,6},{5,7},{6,4},{7,5},{8,10},{9,11},{10,... | collective-permute-start | bytes 196616 | tf_op jit(solution)/shard_map/ppermute | solution.py:32
  59.6 5.0 %collective-permute-start.8 = (f32[64,256]{1,0:T(8,128)S(1)}, f32[64,256]{1,0:T(8,128)S(1)}, u32[]{:S(2)}, u32[]{:S(2)}) collective-permute-start(f32[64,256]{1,0:T(8,128)S(1)} %slice_add_fusion.13), channel_id=1, source_target_pairs={{0,1},{1,0},{2,3},{3,2},{4,5},{5,4},{6,7},{7,6},{8,9},{9,8},{10,11... | collective-permute-start | bytes 196616 | tf_op jit(solution)/shard_map/ppermute | solution.py:32
  61.1 4.4 %collective-permute-start.20 = (f32[64,256]{1,0:T(8,128)S(1)}, f32[64,256]{1,0:T(8,128)S(1)}, u32[]{:S(2)}, u32[]{:S(2)}) collective-permute-start(f32[64,256]{1,0:T(8,128)S(1)} %slice_add_fusion.9), channel_id=1, source_target_pairs={{0,1},{1,0},{2,3},{3,2},{4,5},{5,4},{6,7},{7,6},{8,9},{9,8},{10,11... | collective-permute-start | bytes 196616 | tf_op jit(solution)/shard_map/ppermute | solution.py:32
  64.6 5.2 %collective-permute-start.9 = (f32[64,256]{1,0:T(8,128)S(1)}, f32[64,256]{1,0:T(8,128)S(1)}, u32[]{:S(2)}, u32[]{:S(2)}) collective-permute-start(f32[64,256]{1,0:T(8,128)S(1)} %fusion.181), channel_id=1, source_target_pairs={{0,2},{1,3},{2,0},{3,1},{4,6},{5,7},{6,4},{7,5},{8,10},{9,11},{10,... | collective-permute-start | bytes 196616 | tf_op jit(solution)/shard_map/ppermute | solution.py:32
  65.6 8.1 %collective-permute-start.21 = (f32[64,256]{1,0:T(8,128)S(1)}, f32[64,256]{1,0:T(8,128)S(1)}, u32[]{:S(2)}, u32[]{:S(2)}) collective-permute-start(f32[64,256]{1,0:T(8,128)S(1)} %fusion.177), channel_id=1, source_target_pairs={{0,2},{1,3},{2,0},{3,1},{4,6},{5,7},{6,4},{7,5},{8,10},{9,11},{10,... | collective-permute-start | bytes 196616 | tf_op jit(solution)/shard_map/ppermute | solution.py:32
  71.1 4.3 %collective-permute-start.10 = (f32[64,256]{1,0:T(8,128)S(1)}, f32[64,256]{1,0:T(8,128)S(1)}, u32[]{:S(2)}, u32[]{:S(2)}) collective-permute-start(f32[64,256]{1,0:T(8,128)S(1)} %slice_add_fusion.12), channel_id=1, source_target_pairs={{0,1},{1,0},{2,3},{3,2},{4,5},{5,4},{6,7},{7,6},{8,9},{9,8},{10,11... | collective-permute-start | bytes 196616 | tf_op jit(solution)/shard_map/ppermute | solution.py:32
  75.0 4.3 %collective-permute-start.22 = (f32[64,256]{1,0:T(8,128)S(1)}, f32[64,256]{1,0:T(8,128)S(1)}, u32[]{:S(2)}, u32[]{:S(2)}) collective-permute-start(f32[64,256]{1,0:T(8,128)S(1)} %slice_add_fusion.8), channel_id=1, source_target_pairs={{0,1},{1,0},{2,3},{3,2},{4,5},{5,4},{6,7},{7,6},{8,9},{9,8},{10,11... | collective-permute-start | bytes 196616 | tf_op jit(solution)/shard_map/ppermute | solution.py:32
  75.4 5.2 %collective-permute-start.11 = (f32[64,256]{1,0:T(8,128)S(1)}, f32[64,256]{1,0:T(8,128)S(1)}, u32[]{:S(2)}, u32[]{:S(2)}) collective-permute-start(f32[64,256]{1,0:T(8,128)S(1)} %fusion.180), channel_id=1, source_target_pairs={{0,2},{1,3},{2,0},{3,1},{4,6},{5,7},{6,4},{7,5},{8,10},{9,11},{10,... | collective-permute-start | bytes 196616 | tf_op jit(solution)/shard_map/ppermute | solution.py:32
  79.3 7.0 %collective-permute-start.23 = (f32[64,256]{1,0:T(8,128)S(1)}, f32[64,256]{1,0:T(8,128)S(1)}, u32[]{:S(2)}, u32[]{:S(2)}) collective-permute-start(f32[64,256]{1,0:T(8,128)S(1)} %fusion.176), channel_id=1, source_target_pairs={{0,2},{1,3},{2,0},{3,1},{4,6},{5,7},{6,4},{7,5},{8,10},{9,11},{10,... | collective-permute-start | bytes 196616 | tf_op jit(solution)/shard_map/ppermute | solution.py:32
  81.4 13.7 %collective-permute-start.15 = (f32[16,2048]{1,0:T(8,128)S(1)}, f32[16,2048]{1,0:T(8,128)S(1)}, u32[]{:S(2)}, u32[]{:S(2)}) collective-permute-start(f32[16,2048]{1,0:T(8,128)S(1)} %get-tuple-element.32), channel_id=1, source_target_pairs={{0,16},{4,20},{8,24},{12,28},{16,0},{20,4},{24,8},{28,12},{1,17},{... | collective-permute-start | bytes 393224 | tf_op jit(solution)/shard_map/ppermute | solution.py:111
  83.7 11.4 %collective-permute-start.14 = (f32[16,2048]{1,0:T(8,128)S(1)}, f32[16,2048]{1,0:T(8,128)S(1)}, u32[]{:S(2)}, u32[]{:S(2)}) collective-permute-start(f32[16,2048]{1,0:T(8,128)S(1)} %get-tuple-element.33), channel_id=1, source_target_pairs={{0,20},{4,16},{8,28},{12,24},{16,4},{20,0},{24,12},{28,8},{1,21},{... | collective-permute-start | bytes 393224 | tf_op jit(solution)/shard_map/ppermute | solution.py:111
  83.7 11.2 %collective-permute-start.13 = (f32[16,2048]{1,0:T(8,128)S(1)}, f32[16,2048]{1,0:T(8,128)S(1)}, u32[]{:S(2)}, u32[]{:S(2)}) collective-permute-start(f32[16,2048]{1,0:T(8,128)S(1)} %get-tuple-element.34), channel_id=1, source_target_pairs={{0,24},{4,28},{8,16},{12,20},{16,8},{20,12},{24,0},{28,4},{1,25},{... | collective-permute-start | bytes 393224 | tf_op jit(solution)/shard_map/ppermute | solution.py:111
  85.1 7.6 %collective-permute-start.12 = (f32[16,2048]{1,0:T(8,128)S(1)}, f32[16,2048]{1,0:T(8,128)S(1)}, u32[]{:S(2)}, u32[]{:S(2)}) collective-permute-start(f32[16,2048]{1,0:T(8,128)S(1)} %get-tuple-element.35), channel_id=1, source_target_pairs={{0,28},{4,24},{8,20},{12,16},{16,12},{20,8},{24,4},{28,0},{1,29},{... | collective-permute-start | bytes 393224 | tf_op jit(solution)/shard_map/ppermute | solution.py:111
  87.0 13.8 %collective-permute-start.26 = (f32[16,2048]{1,0:T(8,128)S(1)}, f32[16,2048]{1,0:T(8,128)S(1)}, u32[]{:S(2)}, u32[]{:S(2)}) collective-permute-start(f32[16,2048]{1,0:T(8,128)S(1)} %get-tuple-element.27), channel_id=1, source_target_pairs={{0,4},{4,0},{8,12},{12,8},{16,20},{20,16},{24,28},{28,24},{1,5},{5... | collective-permute-start | bytes 393224 | tf_op jit(solution)/shard_map/ppermute | solution.py:111
  92.7 8.1 %collective-permute-start.25 = (f32[16,2048]{1,0:T(8,128)S(1)}, f32[16,2048]{1,0:T(8,128)S(1)}, u32[]{:S(2)}, u32[]{:S(2)}) collective-permute-start(f32[16,2048]{1,0:T(8,128)S(1)} %get-tuple-element.28), channel_id=1, source_target_pairs={{0,8},{4,12},{8,0},{12,4},{16,24},{20,28},{24,16},{28,20},{1,9},{5... | collective-permute-start | bytes 393224 | tf_op jit(solution)/shard_map/ppermute | solution.py:111
  94.9 5.9 %collective-permute-start.24 = (f32[16,2048]{1,0:T(8,128)S(1)}, f32[16,2048]{1,0:T(8,128)S(1)}, u32[]{:S(2)}, u32[]{:S(2)}) collective-permute-start(f32[16,2048]{1,0:T(8,128)S(1)} %get-tuple-element.29), channel_id=1, source_target_pairs={{0,12},{4,8},{8,4},{12,0},{16,28},{20,24},{24,20},{28,16},{1,13},{... | collective-permute-start | bytes 393224 | tf_op jit(solution)/shard_map/ppermute | solution.py:111
  (1 other events, 2.6 us)
